TPU v7x, 256 devices: a whole 4x4x8 slice. The times are simulated.
256 devices in a mesh: rep: 32 (over z, y), nodes: 8 (over x, core).
Axes of the slice: x: 4, y: 4, z: 8, core: 2. Of those that a mesh axis runs over, the one named last changes fastest.
Arguments:
- adjacency: bfloat16 [32, 512, 16384], P(None, 'nodes', 'rep')
- features: bfloat16 [16384, 50], P(('rep', 'nodes'))
- w_one: float32 [50, 2048], replicated
- w_two: float32 [2048, 121], replicated
- labels: int32 [16384], P(('rep', 'nodes'))
- label_mask: int32 [16384], P(('rep', 'nodes'))
Outputs:
- output 1: float32 [], replicated
- output 2: float32 [50, 2048], replicated
- output 3: float32 [2048, 121], replicated
All inputs are finite; a program needn't handle non-finite values.
Results may differ from a plain program's by a relative error of at most 0.001.
Values are sent between devices in bfloat16 or wider.
A program may use at most 768 MiB of HBM per device.

v0:
```python
import jax
import jax.numpy as jnp
from jax import lax
from jax.sharding import PartitionSpec as P


def solution(mesh):
    all_axes = ("rep", "nodes")
    row_spec = P(("rep", "nodes"))

    def device_step(adj_blk, feat_blk, w_one, w_two, label_blk, mask_blk):
        n_class = w_two.shape[1]
        w_one_lo = w_one.astype(jnp.bfloat16)
        w_two_lo = w_two.astype(jnp.bfloat16)

        def spread(y_blk):
            gathered = lax.all_gather(y_blk, "nodes", axis=0, tiled=True)
            part_sum = lax.dot_general(adj_blk, gathered, (((2,), (0,)), ((), ())), preferred_element_type=jnp.float32)
            return lax.psum_scatter(part_sum, "rep", scatter_dimension=0, tiled=False)

        def collect(g_blk):
            gathered = lax.all_gather(g_blk, "rep", axis=0)
            part_sum = lax.dot_general(adj_blk, gathered, (((0, 1), (0, 1)), ((), ())), preferred_element_type=jnp.float32)
            return lax.psum_scatter(part_sum, "nodes", scatter_dimension=0, tiled=True)

        y_one = jnp.dot(feat_blk, w_one_lo, preferred_element_type=jnp.float32).astype(jnp.bfloat16)
        z_one = spread(y_one)
        h_one = jnp.maximum(z_one, 0.0).astype(jnp.bfloat16)
        y_two = jnp.dot(h_one, w_two_lo, preferred_element_type=jnp.float32).astype(jnp.bfloat16)
        z_two = spread(y_two)
        weights = mask_blk.astype(jnp.float32)
        log_probs = jax.nn.log_softmax(z_two, axis=-1)
        one_hot = (label_blk[:, None] == jnp.arange(n_class)[None, :]).astype(jnp.float32)
        local_sums = jnp.stack([jnp.sum(weights), -jnp.sum(weights * jnp.sum(one_hot * log_probs, axis=-1))])
        global_sums = lax.psum(local_sums, all_axes)
        label_count = global_sums[0]
        loss_value = global_sums[1] / label_count
        g_two = ((jnp.exp(log_probs) - one_hot) * (weights / label_count)[:, None]).astype(jnp.bfloat16)
        dy_two = collect(g_two).astype(jnp.bfloat16)
        dw_two = lax.psum(lax.dot_general(h_one, dy_two, (((0,), (0,)), ((), ())), preferred_element_type=jnp.float32), all_axes)
        dh_one = lax.dot_general(dy_two, w_two_lo, (((1,), (1,)), ((), ())), preferred_element_type=jnp.float32)
        g_one = jnp.where(z_one > 0.0, dh_one, 0.0).astype(jnp.bfloat16)
        dy_one = collect(g_one).astype(jnp.bfloat16)
        dw_one = lax.psum(lax.dot_general(feat_blk, dy_one, (((0,), (0,)), ((), ())), preferred_element_type=jnp.float32), all_axes)
        return loss_value, dw_one, dw_two

    return jax.shard_map(device_step, mesh=mesh, in_specs=(P(None, "nodes", "rep"), row_spec, P(), P(), row_spec, row_spec), out_specs=(P(), P(), P()), check_vma=False)
```

profile of v0, /device:TPU:2, one launch (start us, length us, event | category | flops | bytes accessed | tf_op | source)
XLA Modules:
  0.0 1123.4 jit_solution(355276135241773880)
XLA Ops:
  7.2 0.0 copy-start
  7.2 0.0 all-gather.4.cloned.1.call-start
  7.2 2.1 convolution_convert_fusion
  9.4 0.0 all-gather.4.cloned.1.call-update
  9.4 0.0 reduce-scatter.9.cloned.1.call-start
  9.4 30.5 %all-gather.4.cloned.1.call-done = bf16[512,2048]{1,0:T(8,128)(2,1)} async-done(((bf16[64,2048]{1,0:T(8,128)(2,1)}), bf16[512,2048]{1,0:T(8,128)(2,1)}) %all-gather.4.cloned.1.call-update) | async-done | bytes 2097168 | tf_op jit(solution)/shard_map/all_gather | solution.py:17
  39.9 9.7 convolution_bitcast_fusion
  49.6 0.0 reduce-scatter.9.cloned.1.call-update
  49.6 0.0 reduce-scatter.11.cloned.1.call-start
  49.7 247.7 %reduce-scatter.9.cloned.1.call-done = f32[1,64,2048]{2,1,0:T(8,128)} async-done(((f32[32,64,2048]{2,1,0:T(8,128)}), f32[1,64,2048]{2,1,0:T(8,128)}) %reduce-scatter.9.cloned.1.call-update) | async-done | bytes 524304 | tf_op jit(solution)/shard_map/reduce_scatter | solution.py:19
  297.4 1.3 convolution_convert_fusion.1
  298.6 12.7 %all_gather.17 = bf16[512,121]{1,0:T(8,128)(2,1)S(1)} all-gather(bf16[64,121]{1,0:T(8,128)(2,1)S(1)} %convolution_convert_fusion.1), channel_id=1, replica_groups=mesh['rep'=32,'nodes'=8] {'nodes'}, dimensions={0}, use_global_device_ids=true | all-gather | bytes 139392 | tf_op jit(solution)/shard_map/all_gather | solution.py:17
  311.4 1.7 convolution_bitcast_fusion.3
  313.1 0.0 reduce-scatter.11.cloned.1.call-update
  313.1 0.0 reduce-scatter.13.cloned.1.call-start
  313.1 214.7 %reduce-scatter.11.cloned.1.call-done = f32[1,64,121]{2,1,0:T(8,128)} async-done(((f32[32,64,121]{2,1,0:T(8,128)}), f32[1,64,121]{2,1,0:T(8,128)}) %reduce-scatter.11.cloned.1.call-update) | async-done | bytes 30992 | tf_op jit(solution)/shard_map/reduce_scatter | solution.py:19
  527.9 0.9 reduce_max.10
  528.7 0.9 exponential_reduce_fusion
  529.7 1.0 select_reduce_fusion
  530.7 0.6 convert_reduce_fusion
  531.9 0.7 pad_maximum_fusion
  532.7 73.5 %psum.21 = f32[2]{0:T(128)S(1)} all-reduce(f32[2]{0:T(128)S(1)} %pad_maximum_fusion), channel_id=1, replica_groups=mesh['rep'=32,'nodes'=8] {'rep','nodes'}, use_global_device_ids=true, to_apply=%region_7.8 | all-reduce | flops 2 | bytes 16 | tf_op jit(solution)/shard_map/psum | solution.py:35
  606.1 0.6 fusion.15
  606.7 0.6 convert_divide_fusion
  607.4 0.9 multiply_convert_fusion
  608.3 47.7 %all_gather.18 = bf16[32,64,121]{2,1,0:T(8,128)(2,1)S(1)} all-gather(bf16[1,64,121]{2,1,0:T(8,128)(2,1)S(1)} %multiply_convert_fusion), channel_id=1, replica_groups=mesh['rep'=32,'nodes'=8] {'rep'}, dimensions={0}, use_global_device_ids=true | all-gather | bytes 511104 | tf_op jit(solution)/shard_map/all_gather | solution.py:22
  655.9 0.5 convolution_bitcast_fusion.4
  656.4 0.8 copy.9
  657.2 0.0 reduce-scatter.13.cloned.1.call-update
  657.3 0.0 all-gather.6.cloned.1.call-start
  657.3 28.2 %reduce-scatter.13.cloned.1.call-done = f32[64,121]{1,0:T(8,128)} async-done(((f32[512,121]{1,0:T(8,128)}), f32[64,121]{1,0:T(8,128)}) %reduce-scatter.13.cloned.1.call-update) | async-done | bytes 30992
  685.5 0.9 copy.10
  686.4 2.2 fusion
  688.7 0.0 all-gather.6.cloned.1.call-update
  688.7 0.0 reduce-scatter.15.cloned.1.call-start
  688.7 99.6 %all-gather.6.cloned.1.call-done = bf16[2048,2048]{1,0:T(8,128)(2,1)} async-done(((bf16[64,2048]{1,0:T(8,128)(2,1)}), bf16[2048,2048]{1,0:T(8,128)(2,1)}) %all-gather.6.cloned.1.call-update) | async-done | bytes 8388624 | tf_op jit(solution)/shard_map/all_gather | solution.py:22
  788.3 9.8 convolution_bitcast_fusion.1
  798.1 5.4 copy.11
  803.5 0.0 reduce-scatter.15.cloned.1.call-update
  803.5 0.0 all-reduce.3.cloned.1.call-start
  803.5 1.3 fusion.8
  804.9 32.9 %reduce-scatter.15.cloned.1.call-done = f32[64,2048]{1,0:T(8,128)} async-done(((f32[512,2048]{1,0:T(8,128)}), f32[64,2048]{1,0:T(8,128)}) %reduce-scatter.15.cloned.1.call-update) | async-done | bytes 524304
  837.7 1.3 copy.12
  839.1 1.2 convolution_bitcast_fusion.2
  840.2 0.0 all-reduce.3.cloned.1.call-update
  841.6 269.8 %all-reduce.3.cloned.1.call-done = (f32[50,2048]{1,0:T(8,128)}, f32[2048,121]{1,0:T(8,128)}) async-done(((f32[50,2048]{1,0:T(8,128)}, f32[2048,121]{1,0:T(8,128)}), (f32[50,2048]{1,0:T(8,128)}, f32[2048,121]{1,0:T(8,128)})) %all-reduce.3.cloned.1.call-update) | async-done | bytes 1400848 | tf_op jit(solution)/shard_map/psum | solution.py:44
  1111.3 1.8 copy.15
  1113.2 2.3 copy.16
  (12 shorter events, 0.0 us)
Async XLA Ops:
  7.2 32.8 %copy-start = (bf16[32,64,512]{2,1,0:T(8,128)(2,1)S(1)}, bf16[32,64,512]{2,1,0:T(8,128)(2,1)}, u32[]{:S(2)}) copy-start(bf16[32,64,512]{2,1,0:T(8,128)(2,1)} %param.6) | copy-start | bytes 6291460
  7.2 32.8 %all-gather.4.cloned.1.call-start = ((), (), s32[]{:S(2)}) async-start(), calls=%async_computation.4 | async-start | bytes 2359296 | tf_op jit(solution)/shard_map/all_gather | solution.py:17
  9.4 288.0 %reduce-scatter.9.cloned.1.call-start = ((), (), s32[]{:S(2)}) async-start(), calls=%async_computation.5 | async-start | bytes 17301504 | tf_op jit(solution)/shard_map/reduce_scatter | solution.py:19
  49.6 247.8 %copy-start.2 = (f32[2048,121]{1,0:T(8,128)S(1)}, f32[2048,121]{1,0:T(8,128)}, u32[]{:S(2)}) copy-start(f32[2048,121]{1,0:T(8,128)} %param.9) | copy-start | bytes 2973700
  49.6 478.2 %reduce-scatter.11.cloned.1.call-start = ((), (), s32[]{:S(2)}) async-start(), calls=%async_computation.6 | async-start | bytes 1081344 | tf_op jit(solution)/shard_map/reduce_scatter | solution.py:19
  311.4 218.3 %copy-start.4 = (s32[64]{0:T(128)S(1)}, s32[64]{0:T(128)}, u32[]{:S(2)}) copy-start(s32[64]{0:T(128)} %param.10) | copy-start | bytes 772
  311.4 219.3 %copy-start.5 = (s32[64]{0:T(128)S(1)}, s32[64]{0:T(128)}, u32[]{:S(2)}) copy-start(s32[64]{0:T(128)} %param.11) | copy-start | bytes 772
  313.1 372.4 %reduce-scatter.13.cloned.1.call-start = ((), (), s32[]{:S(2)}) async-start(), calls=%async_computation.8 | async-start | bytes 294912
  608.3 78.2 %copy-start.1 = (f32[1,64,2048]{2,1,0:T(8,128)S(1)}, f32[1,64,2048]{2,1,0:T(8,128)}, u32[]{:S(2)}) copy-start(f32[1,64,2048]{2,1,0:T(8,128)} %reduce-scatter.9.cloned.1.call-done) | copy-start | bytes 1572868
  657.3 131.0 %all-gather.6.cloned.1.call-start = ((), (), s32[]{:S(2)}) async-start(), calls=%async_computation.7 | async-start | bytes 8650752 | tf_op jit(solution)/shard_map/all_gather | solution.py:22
  688.7 149.0 %reduce-scatter.15.cloned.1.call-start = ((), (), s32[]{:S(2)}) async-start(), calls=%async_computation.9 | async-start | bytes 4718592
  803.5 35.6 %copy-start.3 = (bf16[64,50]{0,1:T(8,128)(2,1)S(1)}, bf16[64,50]{0,1:T(8,128)(2,1)}, u32[]{:S(2)}) copy-start(bf16[64,50]{0,1:T(8,128)(2,1)} %param.7) | copy-start | bytes 19204
  803.5 307.8 %all-reduce.3.cloned.1.call-start = ((), (), s32[]{:S(2)}) async-start(), calls=%async_computation.10 | async-start | bytes 3014656 | tf_op jit(solution)/shard_map/psum | solution.py:44
Sparse Core Ops, SparseCore 0:
  10.4 29.4 all-gather.3
  49.8 247.5 reduce-scatter.8
  313.2 214.5 reduce-scatter.10
  657.4 28.0 reduce-scatter.12
  688.8 99.4 all-gather.5
  803.6 34.0 reduce-scatter.14
  843.8 267.5 all-reduce.2
where the time goes:
time: 1120 us
  waiting for transfers between devices  923 us (82%)
  blocking collectives  134 us (12%)
  matrix products  29.8 us (3%)
  between operations  17.3 us (2%)
  local copies, waits for them, and re-layouts  13.1 us (1%)
    reduce_scatter x2, waiting for transfers between devices, spread(): return lax.psum_scatter(part_sum, 'rep', scatter_dimension=0, tiled=False)  462 us
    psum x1, waiting for transfers between devices, device_step(): lax.psum(lax.dot_general(feat_blk, dy_one, (((0,), (0,)), ((), ())), pref...  270 us
    all_gather x1, waiting for transfers between devices, collect(): gathered = lax.all_gather(g_blk, 'rep', axis=0)  99.6 us
    psum x1, blocking collectives, device_step(): global_sums = lax.psum(local_sums, all_axes)  73.5 us
    unnamed x9, waiting for transfers between devices  61.2 us
    all_gather x1, blocking collectives, collect(): gathered = lax.all_gather(g_blk, 'rep', axis=0)  47.7 us
    all_gather x1, waiting for transfers between devices, spread(): gathered = lax.all_gather(y_blk, 'nodes', axis=0, tiled=True)  30.5 us
  transfers between devices with their start and end apart: 7, of which 7 were waited for; matrix products, arithmetic and copies ran while one was open for 0% of the time, Pallas kernels for 0%

commit v1 on v0

v1 whole, which is shorter than its diff:
```python
import functools

import jax
import jax.numpy as jnp
from jax import lax
from jax.experimental import pallas as pl
from jax.experimental.pallas import tpu as pltpu
from jax.sharding import PartitionSpec as P

Y_DIM = 4
X_DIM = 4
CORES = 2
LANES = 128
NSUB = 2
BF = jnp.bfloat16
F32 = jnp.float32


def _step(dims, a_hbm, xs, lab, w1, w2, w2t, dw1_out, dw2_out, loss_out,
          af, xp, y1, cs, cr, sb, rb, z1, h1, y2, yp, zp, zr, g2, gr, dp, rc, rx, ry, g1, gz, gt, dy, rcy, rx1, rx2,
          wb, rwc, rwx, rwy, sy, rwz, fz, oz, oy, ox, oc, ssem, rsem, rsem_a, rsem_b, rsem_f, rsem_ring, rsem_ag, rsem_x):
    Z, Y, X, C, S, CB, H, F, NC = dims
    I = X * C
    NP = Y * I
    HR = H // (2 * NSUB)
    HB = H // Y
    HU = HB // 2
    NCH = Y * S
    rid = lax.axis_index("rep")
    nid = lax.axis_index("nodes")
    z, y, x, c = rid // Y, rid % Y, nid // C, nid % C
    me = y * I + nid
    partner = (rid, x * C + 1 - c)

    def at_z(zz):
        return (zz * Y + y, nid)

    def at_y(yy):
        return (z * Y + yy, nid)

    def at_x(xx):
        return (rid, xx * C + c)

    def send(src, dst, ss, rs, dev):
        pltpu.make_async_remote_copy(src_ref=src, dst_ref=dst, send_sem=ss, recv_sem=rs, device_id=dev,
                                     device_id_type=pl.DeviceIdType.MESH).start()

    def arrived(ref, rs):
        pltpu.make_async_remote_copy(src_ref=ref, dst_ref=ref, send_sem=ssem.at[0], recv_sem=rs, device_id=partner,
                                     device_id_type=pl.DeviceIdType.MESH).wait_recv()

    def sent(ref, ss):
        pltpu.make_async_remote_copy(src_ref=ref, dst_ref=ref, send_sem=ss, recv_sem=rsem.at[0], device_id=partner,
                                     device_id_type=pl.DeviceIdType.MESH).wait_send()

    def dot(a, b):
        return jnp.dot(a, b, preferred_element_type=F32)

    (E_X, E_A, E_B, E_F, E_RING, E_CNT, E_Y2, E_Z2, E_G2, E_DC, E_DX, E_DY, E_G1, E_AG, E_RC0, E_RC1, E_RX, E_WC, E_WX, E_WY, E_WZ,
     E_OZ, E_OY, E_OX, E_OC, E_RX2, E_LOAD) = range(27)

    load = pltpu.make_async_copy(a_hbm, af.at[y], ssem.at[E_LOAD])
    load.start()

    bar = pltpu.get_barrier_semaphore()

    def greet_plane(d, u):
        p = lax.rem(me + d, NP)
        pl.semaphore_signal(bar, inc=1, device_id=(z * Y + p // I, p % I), device_id_type=pl.DeviceIdType.MESH)
        return u

    lax.fori_loop(1, NP, greet_plane, 0)
    for d in range(1, Z):
        pl.semaphore_signal(bar, inc=1, device_id=at_z((z + d) % Z), device_id_type=pl.DeviceIdType.MESH)
    pl.semaphore_wait(bar, NP - 1 + Z - 1)

    def send_x(d, u):
        p = lax.rem(me + d, NP)
        send(xs, xp.at[me], ssem.at[E_X], rsem.at[E_X], (z * Y + p // I, p % I))
        return u

    lax.fori_loop(1, NP, send_x, 0)
    xp[me] = xs[...]
    load.wait()

    order = []
    for k in range(1, Z // 2 + 1):
        order.append(-k)
        if k < Z // 2:
            order.append(k)
    order.append(0)
    for k in order:
        zc = (z + k + Z) % Z
        for d in (1, 3, 2):
            yq = (y + d) % Y
            send(af.at[y, zc, yq], af.at[y, zc, yq], ssem.at[E_A], rsem_a.at[d - 1, zc], at_y(yq))
    for d in (1, 3):
        yq = (y + d) % Y
        for k in range(1, Y):
            ya = (yq + k) % Y
            send(af.at[y, :, ya], af.at[y, :, ya], ssem.at[E_B], rsem_b.at[d // 2, k - 1], at_y(yq))

    arrived(xp.at[pl.ds(0, NP - 1)], rsem.at[E_X])
    HT = HR

    def y1_tile(t, u):
        yb = t // (H // HT)
        col = pl.multiple_of((t % (H // HT)) * HT, HT)
        rows = xp[pl.ds(yb * I, I)].reshape(CB, LANES)
        y1[pl.ds(pl.multiple_of(yb * CB, CB), CB), pl.ds(col, HT)] = dot(rows, w1[:, pl.ds(col, HT)]).astype(BF)
        return u

    lax.fori_loop(0, Y * (H // HT), y1_tile, 0)

    lane = lax.broadcasted_iota(jnp.int32, (S, LANES), 1)
    counted = jnp.sum(xp[...].astype(F32).reshape(NP * S, LANES), axis=0, keepdims=True)
    counted = jnp.sum(jnp.where(lane[0:1] == F, counted, 0.0), axis=1, keepdims=True)
    cs[...] = jnp.broadcast_to(counted, (8, LANES))
    cr[z] = cs[...]
    for d in range(1, Z):
        zq = (z + d) % Z
        send(cs, cr.at[z], ssem.at[E_CNT], rsem.at[E_CNT], at_z(zq))

    def wait_a(zc):
        for d in range(1, Y):
            arrived(af.at[0, 0, 0], rsem_a.at[d - 1, zc])

    def ring(t, u):
        s, j = t // (2 * NSUB), t % (2 * NSUB)
        up = j < NSUB
        dest = lax.rem(jnp.where(up, z - 1 - s, z + 1 + s) + 2 * Z, Z)
        nb = lax.rem(jnp.where(up, z + 1, z - 1) + Z, Z)
        col = pl.multiple_of(j * HR, HR)
        fresh = ((j == 0) & ((s < Z // 2) | (s == Z - 1))) | ((j == NSUB) & (s < Z // 2 - 1))

        @pl.when(fresh)
        def _():
            wait_a(dest)

        acc = dot(af[0, dest, y], y1[pl.ds(0, CB), pl.ds(col, HR)])
        for yb in range(1, Y):
            acc = acc + dot(af[yb, dest, y], y1[pl.ds(yb * CB, CB), pl.ds(col, HR)])
        z1[:, pl.ds(col, HR)] = acc

        @pl.when(s > 0)
        def _():
            prev = jnp.maximum(s - 1, 0)
            arrived(rb.at[0, 0], rsem_ring.at[j, prev])
            z1[:, pl.ds(col, HR)] = z1[:, pl.ds(col, HR)] + rb[j, prev]

        @pl.when(s < Z - 1)
        def _():
            here = jnp.minimum(s, Z - 2)
            sb[j, here] = z1[:, pl.ds(col, HR)]
            send(sb.at[j, here], rb.at[j, here], ssem.at[E_RING], rsem_ring.at[j, here], at_z(nb))

        return u

    lax.fori_loop(0, Z * 2 * NSUB, ring, 0)

    h1[...] = jnp.maximum(z1[...], 0.0).astype(BF)
    y2[...] = dot(h1[...], w2[...]).astype(BF)

    def send_y2(d, u):
        p = lax.rem(me + d, NP)
        send(y2, yp.at[me], ssem.at[E_Y2], rsem.at[E_Y2], (z * Y + p // I, p % I))
        return u

    lax.fori_loop(1, NP, send_y2, 0)
    yp[me] = y2[...]
    arrived(yp.at[pl.ds(0, NP - 1)], rsem.at[E_Y2])
    for yb in range(Y):
        part = dot(af[yb, :, y].reshape(Z * S, CB), yp[yb * I:(yb + 1) * I].reshape(CB, LANES)).reshape(Z, S, LANES)
        zp[...] = part if yb == 0 else zp[...] + part
    for d in range(1, Z):
        zq = (z + d) % Z
        send(zp.at[zq], zr.at[z], ssem.at[E_Z2], rsem.at[E_Z2], at_z(zq))
    zr[z] = zp[z]
    for d in (1, 3):
        for k in range(1, Y):
            arrived(af.at[0, :, 0], rsem_b.at[d // 2, k - 1])
    half = Z // 2
    for d in (1, 3):
        ys, yq = (y - d + Y) % Y, (y + d) % Y
        lo = 0 if d == 1 else half
        for k in range(1, Y):
            ya = (yq + k) % Y
            send(af.at[ys, pl.ds(lo, half), ya], af.at[ys, pl.ds(lo, half), ya], ssem.at[E_F], rsem_f.at[d // 2, k - 1], at_y(yq))
    arrived(zr.at[pl.ds(0, Z - 1)], rsem.at[E_Z2])
    z2 = zr[0]
    for k in range(1, Z):
        z2 = z2 + zr[k]

    arrived(cr.at[pl.ds(0, Z - 1)], rsem.at[E_CNT])
    total = cr[0]
    for k in range(1, Z):
        total = total + cr[k]
    count = total[0:1, 0:1]
    weights = jnp.sum(jnp.where(lane == F, xs[...].astype(F32), 0.0), axis=1, keepdims=True)
    real = lane < NC
    top = jnp.max(jnp.where(real, z2, -jnp.inf), axis=1, keepdims=True)
    shifted = jnp.where(real, z2 - top, 0.0)
    log_probs = shifted - jnp.log(jnp.sum(jnp.where(real, jnp.exp(shifted), 0.0), axis=1, keepdims=True))
    hot = lab[...] == lane
    picked = jnp.sum(jnp.where(hot, log_probs, 0.0), axis=1, keepdims=True)
    loss_part = -jnp.sum(weights * picked, axis=0, keepdims=True)
    diff = jnp.where(real, jnp.exp(log_probs), 0.0) - hot.astype(F32)
    g2[...] = (diff * (weights / count)).astype(BF)
    for d in range(1, Z):
        zq = (z + d) % Z
        send(g2, gr.at[z], ssem.at[E_G2], rsem.at[E_G2], at_z(zq))
    gr[z] = g2[...]
    arrived(gr.at[pl.ds(0, Z - 1)], rsem.at[E_G2])

    g2t = gr[...].reshape(Z * S, LANES).T
    for yb in range(Y):
        part = dot(g2t, af[yb, :, y].reshape(Z * S, CB))
        dp[yb] = part.T.reshape(X, C, S, LANES)
    send(dp.at[:, :, 1 - c], rc, ssem.at[E_DC], rsem.at[E_DC], partner)
    arrived(rc, rsem.at[E_DC])
    rc[...] = rc[...] + dp[:, :, c]
    for d in range(1, X):
        xq = (x + d) % X
        send(rc.at[:, xq], rx.at[x], ssem.at[E_DX], rsem.at[E_DX], at_x(xq))
    rx[x] = rc[:, x]
    arrived(rx.at[pl.ds(0, X - 1)], rsem.at[E_DX])
    acc = rx[0]
    for k in range(1, X):
        acc = acc + rx[k]
    rx[x] = acc
    for d in range(1, Y):
        yq = (y + d) % Y
        send(rx.at[x, yq], ry.at[y], ssem.at[E_DY], rsem.at[E_DY], at_y(yq))
    ry[y] = rx[x, y]
    arrived(ry.at[pl.ds(0, Y - 1)], rsem.at[E_DY])
    acc = ry[0]
    for k in range(1, Y):
        acc = acc + ry[k]
    dy2 = acc.astype(BF)

    for yb in range(Y):
        for v in range(2):
            col = yb * HB + v * HU
            dh = dot(dy2, w2t[:, col:col + HU])
            g1[yb, v] = jnp.where(z1[:, col:col + HU] > 0.0, dh, 0.0).astype(BF)
    for v in range(2):
        for d in range(1, Y):
            yq = (y + d) % Y
            send(g1.at[yq, v], gz.at[v, z, y], ssem.at[E_G1], rsem_x.at[v, 0], at_y(yq))
        gz[v, z, y] = g1[y, v]
    mark = (lax.broadcasted_iota(jnp.int32, (HB, LANES), 0) == 0) & (lax.broadcasted_iota(jnp.int32, (HB, LANES), 1) == NC)
    for k in range(Y):
        part = lax.dot_general(h1[:, k * HB:(k + 1) * HB], dy2, (((0,), (0,)), ((), ())), preferred_element_type=F32)
        if k == 0:
            part = jnp.where(mark, loss_part, part)
        per = HB // (Y * Z * 8)
        rows = part.reshape(per, Y, Z, 8, LANES)
        for m in range(per):
            q = k * per + m
            wb[q // X, q % X, pl.ds(0, Y)] = rows[m]
    for v in range(2):
        arrived(gz.at[v, 0, pl.ds(0, Y - 1)], rsem_x.at[v, 0])
    for t in range(1, half + 1):
        for v in range(2):
            for d in range(2):
                sgn = 1 if d == 0 else -1
                blk = (z - sgn * (t - 1) + Z) % Z
                if t > 1:
                    arrived(gz.at[v, 0], rsem_ag.at[v, d, t - 1])
                ref = gz.at[v, blk]
                if t == half:
                    ref = gz.at[v, blk, pl.ds(d * (Y // 2), Y // 2)]
                send(ref, ref, ssem.at[E_AG], rsem_ag.at[v, d, t], at_z((z + sgn + Z) % Z))
    for d in (1, 3):
        for k in range(1, Y):
            arrived(af.at[0, pl.ds(0, half), 0], rsem_f.at[d // 2, k - 1])

    def dy1_chunk(v):
        def body(q, u):
            yb = q * NCH // CB
            off = pl.multiple_of((q % (CB // NCH)) * NCH, NCH)
            dy[v, q // C, q % C] = dot(gt[...], af[yb, :, :, :, pl.ds(off, NCH)].reshape(Z * Y * S, NCH))
            return u
        return body

    for v in range(2):
        for d in range(2):
            arrived(gz.at[v, 0, pl.ds(0, Y // 2)], rsem_ag.at[v, d, half])
        for k in range(Z):
            gt[:, k * Y * S:(k + 1) * Y * S] = gz[v, k].reshape(Y * S, HU).T
        lax.fori_loop(0, X * C, dy1_chunk(v), 0)
        send(dy.at[v, :, 1 - c], rcy.at[v], ssem.at[E_RC0 + v], rsem.at[E_RC0 + v], partner)
    nxt, prv, opp = (x + 1) % X, (x + X - 1) % X, (x + 2) % X
    hh = HU // 2
    for v in range(2):
        arrived(rcy.at[v], rsem.at[E_RC0 + v])
        for k in range(X):
            rcy[v, k] = rcy[v, k] + dy[v, k, c]
        send(rcy.at[v, opp, pl.ds(0, hh)], rx1.at[v, 0], ssem.at[E_RX], rsem_x.at[v, 1], at_x(nxt))
        send(rcy.at[v, opp, pl.ds(hh, hh)], rx1.at[v, 1], ssem.at[E_RX], rsem_x.at[v, 2], at_x(prv))
    for v in range(2):
        arrived(rx1.at[v, 0], rsem_x.at[v, 1])
        rcy[v, nxt, pl.ds(0, hh)] = rcy[v, nxt, pl.ds(0, hh)] + rx1[v, 0]
        send(rcy.at[v, nxt], rx2.at[v, 0], ssem.at[E_RX2], rsem_x.at[v, 3], at_x(nxt))
        arrived(rx1.at[v, 1], rsem_x.at[v, 2])
        rcy[v, prv, pl.ds(hh, hh)] = rcy[v, prv, pl.ds(hh, hh)] + rx1[v, 1]
        send(rcy.at[v, prv], rx2.at[v, 1], ssem.at[E_RX2], rsem_x.at[v, 4], at_x(prv))
    xn = xp[pl.ds(nid * Y, Y)].reshape(NCH, LANES)
    for v in range(2):
        arrived(rx2.at[v, 0], rsem_x.at[v, 3])
        arrived(rx2.at[v, 1], rsem_x.at[v, 4])
        acc = rcy[v, x] + rx2[v, 0] + rx2[v, 1]
        part = dot(acc.astype(BF), xn)
        per = HU // (Z * 8)
        rows = part.reshape(per, Z, 8, LANES)
        for m in range(per):
            q = v * per + m
            wb[q // X, q % X, Y] = rows[m]

    send(wb.at[1 - c], rwc, ssem.at[E_WC], rsem.at[E_WC], partner)
    arrived(rwc, rsem.at[E_WC])
    rwc[...] = rwc[...] + wb[c]
    for d in range(1, X):
        xq = (x + d) % X
        send(rwc.at[xq], rwx.at[x], ssem.at[E_WX], rsem.at[E_WX], at_x(xq))
    rwx[x] = rwc[x]
    arrived(rwx.at[pl.ds(0, X - 1)], rsem.at[E_WX])
    acc = rwx[0]
    for k in range(1, X):
        acc = acc + rwx[k]
    rwx[x] = acc
    for d in range(1, Y):
        yq = (y + d) % Y
        send(rwx.at[x, yq], rwy.at[y], ssem.at[E_WY], rsem.at[E_WY], at_y(yq))
    rwy[y] = rwx[x, y]
    sy[:, 1] = rwx[x, Y]
    arrived(rwy.at[pl.ds(0, Y - 1)], rsem.at[E_WY])
    acc = rwy[0]
    for k in range(1, Y):
        acc = acc + rwy[k]
    sy[:, 0] = acc
    for d in range(1, Z):
        zq = (z + d) % Z
        send(sy.at[zq], rwz.at[z], ssem.at[E_WZ], rsem.at[E_WZ], at_z(zq))
    rwz[z] = sy[z]
    arrived(rwz.at[pl.ds(0, Z - 1)], rsem.at[E_WZ])
    acc = rwz[0]
    for k in range(1, Z):
        acc = acc + rwz[k]
    fz[...] = acc
    for d in range(1, Z):
        zq = (z + d) % Z
        send(fz, oz.at[z], ssem.at[E_OZ], rsem.at[E_OZ], at_z(zq))
    oz[z] = fz[...]
    arrived(oz.at[pl.ds(0, Z - 1)], rsem.at[E_OZ])
    for d in range(1, Y):
        yq = (y + d) % Y
        send(oz, oy.at[y], ssem.at[E_OY], rsem.at[E_OY], at_y(yq))
    oy[y] = oz[...]
    arrived(oy.at[pl.ds(0, Y - 1)], rsem.at[E_OY])
    for d in range(1, X):
        xq = (x + d) % X
        send(oy, ox.at[x], ssem.at[E_OX], rsem.at[E_OX], at_x(xq))
    ox[x] = oy[...]
    arrived(ox.at[pl.ds(0, X - 1)], rsem.at[E_OX])
    send(ox, oc.at[c], ssem.at[E_OC], rsem.at[E_OC], partner)
    oc[c] = ox[...]
    arrived(oc.at[0], rsem.at[E_OC])

    for k in range(C):
        full = oc[k, :, :, :, 0].reshape(H // C, LANES)
        dw2_out[k * (H // C):(k + 1) * (H // C), :] = full[:, 0:NC]
        if k == 0:
            loss_out[...] = jnp.broadcast_to(full[0:1, NC:NC + 1] / count, (8, LANES))
    for yb in range(Y):
        part = oc[:, :, yb, :, 1].reshape(HB, LANES).T
        dw1_out[:, yb * HB:(yb + 1) * HB] = part[0:F]

    sent(xp.at[pl.ds(0, NP - 1)], ssem.at[E_X])
    sent(af.at[pl.ds(0, Y - 1), :, 0], ssem.at[E_A])
    sent(af.at[pl.ds(0, Y - 1), :, pl.ds(0, 2)], ssem.at[E_B])
    sent(af.at[pl.ds(0, Y - 1), :, 0], ssem.at[E_F])
    sent(sb, ssem.at[E_RING])
    sent(cr.at[pl.ds(0, Z - 1)], ssem.at[E_CNT])
    sent(yp.at[pl.ds(0, NP - 1)], ssem.at[E_Y2])
    sent(zr.at[pl.ds(0, Z - 1)], ssem.at[E_Z2])
    sent(gr.at[pl.ds(0, Z - 1)], ssem.at[E_G2])
    sent(rc, ssem.at[E_DC])
    sent(rx.at[pl.ds(0, X - 1)], ssem.at[E_DX])
    sent(ry.at[pl.ds(0, Y - 1)], ssem.at[E_DY])
    sent(g1.at[pl.ds(0, Y - 1)], ssem.at[E_G1])
    sent(gz.at[:, pl.ds(0, Z - 1)], ssem.at[E_AG])
    sent(rcy.at[0], ssem.at[E_RC0])
    sent(rcy.at[1], ssem.at[E_RC1])
    sent(rx1, ssem.at[E_RX])
    sent(rx2, ssem.at[E_RX2])
    sent(rwc, ssem.at[E_WC])
    sent(rwx.at[pl.ds(0, X - 1)], ssem.at[E_WX])
    sent(rwy.at[pl.ds(0, Y - 1)], ssem.at[E_WY])
    sent(rwz.at[pl.ds(0, Z - 1)], ssem.at[E_WZ])
    sent(oz.at[pl.ds(0, Z - 1)], ssem.at[E_OZ])
    sent(oy.at[pl.ds(0, Y - 1)], ssem.at[E_OY])
    sent(ox.at[pl.ds(0, X - 1)], ssem.at[E_OX])
    sent(oc.at[0], ssem.at[E_OC])


def solution(mesh):
    Y, X, C = Y_DIM, X_DIM, CORES
    Z = mesh.shape["rep"] // Y
    row_spec = P(("rep", "nodes"))

    def device_step(adj_blk, feat_blk, w_one, w_two, label_blk, mask_blk):
        R, S, CB = adj_blk.shape
        F, H = w_one.shape
        NC = w_two.shape[1]
        I = X * C
        NP = Y * I
        HR = H // (2 * NSUB)
        HB = H // Y
        HU = HB // 2
        NCH = Y * S
        assert R == Z * Y and CB == S * I and F < LANES and NC < LANES
        xs = jnp.concatenate([feat_blk, mask_blk[:, None].astype(BF), jnp.zeros((S, LANES - F - 1), BF)], axis=1)
        w1 = jnp.pad(w_one, ((0, LANES - F), (0, 0))).astype(BF)
        w2 = jnp.pad(w_two, ((0, 0), (0, LANES - NC))).astype(BF)
        vm = pltpu.VMEM
        dma = pltpu.SemaphoreType.DMA
        scratch = [
            vm((Y, Z, Y, S, CB), BF),
            vm((NP, S, LANES), BF),
            vm((Y * CB, H), BF),
            vm((8, LANES), F32),
            vm((Z, 8, LANES), F32),
            vm((2 * NSUB, Z - 1, S, HR), F32),
            vm((2 * NSUB, Z - 1, S, HR), F32),
            vm((S, H), F32),
            vm((S, H), BF),
            vm((S, LANES), BF),
            vm((NP, S, LANES), BF),
            vm((Z, S, LANES), F32),
            vm((Z, S, LANES), F32),
            vm((S, LANES), BF),
            vm((Z, S, LANES), BF),
            vm((Y, X, C, S, LANES), F32),
            vm((Y, X, S, LANES), F32),
            vm((X, Y, S, LANES), F32),
            vm((Y, S, LANES), F32),
            vm((Y, 2, S, HU), BF),
            vm((2, Z, Y, S, HU), BF),
            vm((HU, Z * Y * S), BF),
            vm((2, X, C, HU, NCH), F32),
            vm((2, X, HU, NCH), F32),
            vm((2, 2, HU // 2, NCH), F32),
            vm((2, 2, HU, NCH), F32),
            vm((C, X, Y + 1, Z, 8, LANES), F32),
            vm((X, Y + 1, Z, 8, LANES), F32),
            vm((X, Y + 1, Z, 8, LANES), F32),
            vm((Y, Z, 8, LANES), F32),
            vm((Z, 2, 8, LANES), F32),
            vm((Z, 2, 8, LANES), F32),
            vm((2, 8, LANES), F32),
            vm((Z, 2, 8, LANES), F32),
            vm((Y, Z, 2, 8, LANES), F32),
            vm((X, Y, Z, 2, 8, LANES), F32),
            vm((C, X, Y, Z, 2, 8, LANES), F32),
            dma((27,)),
            dma((25,)),
            dma((Y - 1, Z)),
            dma((2, Y - 1)),
            dma((2, Y - 1)),
            dma((2 * NSUB, Z - 1)),
            dma((2, 2, Z // 2 + 1)),
            dma((2, 5)),
        ]
        vspec = pl.BlockSpec(memory_space=pltpu.VMEM)
        dw_one, dw_two, loss = pl.pallas_call(
            functools.partial(_step, (Z, Y, X, C, S, CB, H, F, NC)),
            out_shape=(jax.ShapeDtypeStruct((F, H), F32), jax.ShapeDtypeStruct((H, NC), F32), jax.ShapeDtypeStruct((8, LANES), F32)),
            in_specs=[pl.BlockSpec(memory_space=pl.ANY)] + [vspec] * 5,
            out_specs=(vspec, vspec, vspec),
            scratch_shapes=scratch,
            compiler_params=pltpu.CompilerParams(collective_id=0, has_side_effects=True, vmem_limit_bytes=60 * 1024 * 1024),
            name="gcn_step",
        )(adj_blk.reshape(Z, Y, S, CB), xs, label_blk[:, None], w1, w2, w2.T)
        return loss[0, 0], dw_one, dw_two

    return jax.shard_map(device_step, mesh=mesh, in_specs=(P(None, "nodes", "rep"), row_spec, P(), P(), row_spec, row_spec), out_specs=(P(), P(), P()), check_vma=False)
```

time: 1120 us -> 224 us (0.20)
  waiting for transfers between devices: 923 us -> 0 us
  Pallas kernels: 0 us -> 206 us
  blocking collectives: 134 us -> 0 us
  matrix products: 29.8 us -> 0 us
  between operations: 17.3 us -> 0.66 us
    reduce_scatter x2 -> x0, waiting for transfers between devices: 462 us -> none  [spread(): return lax.psum_scatter(part_sum, 'rep', scatter_dimension=0, tiled=False)]
    psum x1 -> x0, waiting for transfers between devices: 270 us -> none  [device_step(): lax.psum(lax.dot_general(feat_blk, dy_one, (((0,), (0,)), ((), ())), pref...]
    pallas_call x0 -> x1, Pallas kernels: none -> 206 us  [device_step(): pl.pallas_call(functools.partial(_step, (Z, Y, X, C, S, CB, H, F, NC)), o...]
    all_gather x2 -> x0, waiting for transfers between devices: 130 us -> none  [the longest x1 99.6 us: collect(): gathered = lax.all_gather(g_blk, 'rep', axis=0)]
    psum x1 -> x0, blocking collectives: 73.5 us -> none  [device_step(): global_sums = lax.psum(local_sums, all_axes)]
    unnamed x9 -> x0, waiting for transfers between devices: 61.2 us -> none
    all_gather x2 -> x0, blocking collectives: 60.4 us -> none  [the longest x1 47.7 us: collect(): gathered = lax.all_gather(g_blk, 'rep', axis=0)]
    dot_general x9 -> x0, matrix products: 29.8 us -> none  [the longest x2 11.4 us: spread(): lax.dot_general(adj_blk, gathered, (((2,), (0,)), ((), ())), preferred_el...]
  transfers between devices with their start and end apart: 7 -> 0, of which waited for: 7 -> 0; matrix products, arithmetic and copies ran while one was open for 0% -> 0% of each run, Pallas kernels for 0% -> 0%
where the time goes in v1:
time: 224 us; the launch traced here: 221 us
  Pallas kernels  206 us (92%)
  local copies, waits for them, and re-layouts  10.9 us (5%)
  other arithmetic  2.48 us (1%)
    pallas_call x1, Pallas kernels, device_step(): pl.pallas_call(functools.partial(_step, (Z, Y, X, C, S, CB, H, F, NC)), o...  206 us
    unnamed x7, local copies, waits for them, and re-layouts  5.56 us

profile of v1, /device:TPU:2, one launch (start us, length us, event | category | flops | bytes accessed | tf_op | source)
XLA Modules:
  0.0 220.5 jit_solution(2748759005224204215)
XLA Ops:
  0.6 0.0 copy-start
  0.6 0.7 convert_bitcast_fusion
  1.4 0.1 pad.14.clone
  1.5 0.1 copy.10
  1.6 0.8 copy.9
  2.4 0.7 maximum_maximum_fusion.xs
  3.1 1.4 copy.12.lab
  4.4 1.0 convert.8
  5.5 0.8 pad.10.w1
  6.3 0.0 copy-done
  6.3 0.4 copy.11
  6.7 0.3 copy.14
  7.0 0.9 pad_bitcast_fusion.w2t
  7.8 0.9 pad.11.clone.w2
  8.8 206.5 %gcn_step.1 = (f32[50,2048]{1,0:T(8,128)}, f32[2048,121]{1,0:T(8,128)}, f32[8,128]{1,0:T(8,128)}) custom-call(bf16[8,4,64,512]{3,2,1,0:T(8,128)(2,1)} %bitcast.7, bf16[64,128]{1,0:T(8,128)(2,1)} %maximum_maximum_fusion.xs, s32[64,1]{1,0:T(8,128)} %copy.12.lab, bf16[128,2048]{1,0:T(8,128)(2,1)} %pad.10.w1, bf16[2048,128]{1,0:T(8,128)(2,1)} %pad.11.clone.w2, ...), custom_call_target="tpu_custom_call" | custom-call | tf_op jit(solution)/shard_map/gcn_step/pallas_call | solution.py:476
  215.3 1.2 slice.3
  216.5 1.8 copy.17
  218.3 2.3 %copy.18 = f32[2048,121]{1,0:T(8,128)} copy(f32[2048,121]{1,0:T(8,128)} %get-tuple-element.14) | data formatting | bytes 1982464
  (1 shorter events, 0.0 us)
Async XLA Ops:
  0.6 5.7 %copy-start = (f32[2048,121]{1,0:T(8,128)S(1)}, f32[2048,121]{1,0:T(8,128)}, u32[]{:S(2)}) copy-start(f32[2048,121]{1,0:T(8,128)} %param.9) | copy-start | bytes 2973700

commit v2 on v1

v2 whole, which is shorter than its diff:
```python
import functools

import jax
import jax.numpy as jnp
from jax import lax
from jax.experimental import pallas as pl
from jax.experimental.pallas import tpu as pltpu
from jax.sharding import PartitionSpec as P

Y_DIM = 4
X_DIM = 4
CORES = 2
LANES = 128
NSUB = 2
NV = 4
NSEM = 36
BF = jnp.bfloat16
F32 = jnp.float32


def _step(dims, a_hbm, feat, lab, msk, w_one, w_two, dw1_out, dw2_out, loss_out,
          af, mt, mtt, w1f, w2f, w1, w2, w2t, xs, xp, y1, cs, cr, sb, rb, z1, h1, y2, yp, zp, zr, g2, gr, dp, rc, rx, ry,
          g1, gz, gt, dy, rcy, rx1, rx2, wb, wc, wx, wy, wz, wf, oz, oy, ox, oc, pb, pc, px, pz, pf, qz, qy, qx,
          ssem, rsem, rsem_a, rsem_b, rsem_f, rsem_ring, rsem_g, rsem_ag, rsem_c, rsem_x):
    Z, Y, X, C, S, CB, H, F, NC = dims
    I = X * C
    NQ = Y * X
    HR = H // (2 * NSUB)
    HB = H // Y
    HU = HB // NV
    NCH = Y * S
    half = Z // 2
    rid = lax.axis_index("rep")
    nid = lax.axis_index("nodes")
    z, y, x, c = rid // Y, rid % Y, nid // C, nid % C
    chip = y * X + x
    partner = (rid, x * C + 1 - c)

    def at_z(zz):
        return (zz * Y + y, nid)

    def at_y(yy):
        return (z * Y + yy, nid)

    def at_x(xx):
        return (rid, xx * C + c)

    def at_chip(q):
        return (z * Y + q // X, (q % X) * C + c)

    def send(src, dst, ss, rs, dev):
        pltpu.make_async_remote_copy(src_ref=src, dst_ref=dst, send_sem=ss, recv_sem=rs, device_id=dev,
                                     device_id_type=pl.DeviceIdType.MESH).start()

    def arrived(ref, rs):
        pltpu.make_async_remote_copy(src_ref=ref, dst_ref=ref, send_sem=ssem.at[0], recv_sem=rs, device_id=partner,
                                     device_id_type=pl.DeviceIdType.MESH).wait_recv()

    def sent(ref, ss):
        pltpu.make_async_remote_copy(src_ref=ref, dst_ref=ref, send_sem=ss, recv_sem=rsem.at[0], device_id=partner,
                                     device_id_type=pl.DeviceIdType.MESH).wait_send()

    def dot(a, b):
        return jnp.dot(a, b, preferred_element_type=F32)

    def most(ref):
        return ref.at[0, pl.ds(0, NQ - 1)]

    def plane_rows(ref, yb):
        return jnp.stack([ref[k, yb * X:(yb + 1) * X] for k in range(C)], axis=1).reshape(CB, LANES)

    def added(ref, n):
        acc = ref[0]
        for k in range(1, n):
            acc = acc + ref[k]
        return acc

    (E_X, E_XC, E_A, E_B, E_F, E_RING, E_CNT, E_Y2, E_Y2C, E_Z2, E_G2, E_DC, E_DX, E_DY, E_G1, E_AG, E_RC, E_RX, E_RX2,
     E_WC, E_WX, E_WY, E_WZ, E_OZ, E_OY, E_OX, E_OC, E_PC, E_PX, E_PZ, E_QZ, E_QY, E_QX, E_LA, E_L1, E_L2) = range(NSEM)

    load_a = pltpu.make_async_copy(a_hbm, af.at[y], ssem.at[E_LA])
    load_1 = pltpu.make_async_copy(w_one, w1f, ssem.at[E_L1])
    load_2 = pltpu.make_async_copy(w_two, w2f, ssem.at[E_L2])
    load_a.start()
    load_1.start()
    load_2.start()

    bar = pltpu.get_barrier_semaphore()
    for d in range(1, Z):
        pl.semaphore_signal(bar, inc=1, device_id=at_z((z + d) % Z), device_id_type=pl.DeviceIdType.MESH)

    def greet_plane(d, u):
        pl.semaphore_signal(bar, inc=1, device_id=at_chip(lax.rem(chip + d, NQ)), device_id_type=pl.DeviceIdType.MESH)
        return u

    lax.fori_loop(1, NQ, greet_plane, 0)
    pl.semaphore_signal(bar, inc=1, device_id=partner, device_id_type=pl.DeviceIdType.MESH)

    mt[...] = jnp.zeros_like(mt)
    mt[0:F] = feat[...].astype(F32)
    mt[F:F + 1] = msk[...].astype(F32)
    mt[F + 1:F + 2] = lab[...].astype(F32)
    mtt[...] = mt[...].T
    xs[...] = mtt[...].astype(BF)
    pl.semaphore_wait(bar, NQ + Z - 1)

    def send_x(d, u):
        q = lax.rem(chip + d, NQ)
        send(xs, xp.at[c, chip], ssem.at[E_X], rsem.at[E_X], at_chip(q))
        return u

    lax.fori_loop(1, NQ, send_x, 0)
    xp[c, chip] = xs[...]
    load_a.wait()

    order = []
    for k in range(1, half + 1):
        order.append(-k)
        if k < half:
            order.append(k)
    order.append(0)
    for k in order:
        zc = (z + k + Z) % Z
        for d in (1, 3, 2):
            yq = (y + d) % Y
            send(af.at[y, zc, yq], af.at[y, zc, yq], ssem.at[E_A], rsem_a.at[d - 1, zc], at_y(yq))
    for d in (1, 3):
        yq = (y + d) % Y
        for k in range(1, Y):
            ya = (yq + k) % Y
            send(af.at[y, :, ya], af.at[y, :, ya], ssem.at[E_B], rsem_b.at[d // 2, k - 1], at_y(yq))

    load_1.wait()
    w1[...] = jnp.zeros_like(w1)
    w1[0:F] = w1f[...].astype(BF)
    load_2.wait()
    w2[...] = jnp.zeros_like(w2)
    for k in range(Y):
        rows = slice(k * HB, (k + 1) * HB)
        w2[rows, 0:NC] = w2f[rows].astype(BF)
        w2t[:, rows] = w2[rows].T

    arrived(most(xp), rsem.at[E_X])
    send(xp.at[c], xp.at[c], ssem.at[E_XC], rsem.at[E_XC], partner)
    arrived(xp.at[0], rsem.at[E_XC])

    def wait_a(zc):
        for d in range(1, Y):
            arrived(af.at[0, 0, 0], rsem_a.at[d - 1, zc])

    def ring(t, u):
        s, j = t // (2 * NSUB), t % (2 * NSUB)
        up = j < NSUB
        dest = lax.rem(jnp.where(up, z - 1 - s, z + 1 + s) + 2 * Z, Z)
        nb = lax.rem(jnp.where(up, z + 1, z - 1) + Z, Z)
        col = pl.multiple_of(j * HR, HR)
        fresh = ((j == 0) & ((s < half) | (s == Z - 1))) | ((j == NSUB) & (s < half - 1))

        @pl.when(s == 0)
        def _():
            for yb in range(Y):
                rows = plane_rows(xp, yb)
                y1[yb * CB:(yb + 1) * CB, pl.ds(col, HR)] = dot(rows, w1[:, pl.ds(col, HR)]).astype(BF)

        @pl.when(fresh)
        def _():
            wait_a(dest)

        acc = dot(af[0, dest, y], y1[pl.ds(0, CB), pl.ds(col, HR)])
        for yb in range(1, Y):
            acc = acc + dot(af[yb, dest, y], y1[pl.ds(yb * CB, CB), pl.ds(col, HR)])
        z1[:, pl.ds(col, HR)] = acc

        @pl.when(s > 0)
        def _():
            prev = jnp.maximum(s - 1, 0)
            arrived(rb.at[0, 0], rsem_ring.at[j, prev])
            z1[:, pl.ds(col, HR)] = z1[:, pl.ds(col, HR)] + rb[j, prev]

        @pl.when(s < Z - 1)
        def _():
            here = jnp.minimum(s, Z - 2)
            sb[j, here] = z1[:, pl.ds(col, HR)]
            send(sb.at[j, here], rb.at[j, here], ssem.at[E_RING], rsem_ring.at[j, here], at_z(nb))

        return u

    lax.fori_loop(0, Z * 2 * NSUB, ring, 0)

    h1[...] = jnp.maximum(z1[...], 0.0).astype(BF)
    y2[...] = dot(h1[...], w2[...]).astype(BF)

    def send_y2(d, u):
        q = lax.rem(chip + d, NQ)
        send(y2, yp.at[c, chip], ssem.at[E_Y2], rsem.at[E_Y2], at_chip(q))
        return u

    lax.fori_loop(1, NQ, send_y2, 0)
    yp[c, chip] = y2[...]
    lane = lax.broadcasted_iota(jnp.int32, (S, LANES), 1)
    counted = jnp.sum(xp[...].astype(F32).reshape(Y * CB, LANES), axis=0, keepdims=True)
    counted = jnp.sum(jnp.where(lane[0:1] == F, counted, 0.0), axis=1, keepdims=True)
    cs[...] = jnp.broadcast_to(counted, (8, LANES))
    cr[z] = cs[...]
    for d in range(1, Z):
        send(cs, cr.at[z], ssem.at[E_CNT], rsem.at[E_CNT], at_z((z + d) % Z))
    arrived(most(yp), rsem.at[E_Y2])
    send(yp.at[c], yp.at[c], ssem.at[E_Y2C], rsem.at[E_Y2C], partner)
    arrived(yp.at[0], rsem.at[E_Y2C])
    for yb in range(Y):
        part = dot(af[yb, :, y].reshape(Z * S, CB), plane_rows(yp, yb)).reshape(Z, S, LANES)
        zp[...] = part if yb == 0 else zp[...] + part
    for d in range(1, Z):
        zq = (z + d) % Z
        send(zp.at[zq], zr.at[z], ssem.at[E_Z2], rsem.at[E_Z2], at_z(zq))
    zr[z] = zp[z]
    for d in (1, 3):
        for k in range(1, Y):
            arrived(af.at[0, :, 0], rsem_b.at[d // 2, k - 1])
    for d in (1, 3):
        ys, yq = (y - d + Y) % Y, (y + d) % Y
        lo = 0 if d == 1 else half
        for k in range(1, Y):
            ya = (yq + k) % Y
            send(af.at[ys, pl.ds(lo, half), ya], af.at[ys, pl.ds(lo, half), ya], ssem.at[E_F], rsem_f.at[d // 2, k - 1], at_y(yq))
    arrived(zr.at[pl.ds(0, Z - 1)], rsem.at[E_Z2])
    z2 = added(zr, Z)

    arrived(cr.at[pl.ds(0, Z - 1)], rsem.at[E_CNT])
    count = added(cr, Z)[0:1, 0:1]
    own = mtt[...]
    weights = jnp.sum(jnp.where(lane == F, own, 0.0), axis=1, keepdims=True)
    labels = jnp.sum(jnp.where(lane == F + 1, own, 0.0), axis=1, keepdims=True)
    real = lane < NC
    top = jnp.max(jnp.where(real, z2, -jnp.inf), axis=1, keepdims=True)
    shifted = jnp.where(real, z2 - top, 0.0)
    log_probs = shifted - jnp.log(jnp.sum(jnp.where(real, jnp.exp(shifted), 0.0), axis=1, keepdims=True))
    hot = labels == lane.astype(F32)
    picked = jnp.sum(jnp.where(hot, log_probs, 0.0), axis=1, keepdims=True)
    loss_part = -jnp.sum(weights * picked, axis=0, keepdims=True)
    diff = jnp.where(real, jnp.exp(log_probs), 0.0) - hot.astype(F32)
    g2[...] = (diff * (weights / count)).astype(BF)
    for d in range(1, Z):
        send(g2, gr.at[z], ssem.at[E_G2], rsem.at[E_G2], at_z((z + d) % Z))
    gr[z] = g2[...]
    arrived(gr.at[pl.ds(0, Z - 1)], rsem.at[E_G2])

    g2t = gr[...].reshape(Z * S, LANES).T
    for yb in range(Y):
        part = dot(g2t, af[yb, :, y].reshape(Z * S, CB))
        dp[yb] = part.T.reshape(X, C, S, LANES)
    send(dp.at[:, :, 1 - c], rc, ssem.at[E_DC], rsem.at[E_DC], partner)
    arrived(rc, rsem.at[E_DC])
    rc[...] = rc[...] + dp[:, :, c]
    for d in range(1, X):
        xq = (x + d) % X
        send(rc.at[:, xq], rx.at[x], ssem.at[E_DX], rsem.at[E_DX], at_x(xq))
    rx[x] = rc[:, x]
    arrived(rx.at[pl.ds(0, X - 1)], rsem.at[E_DX])
    rx[x] = added(rx, X)
    for d in range(1, Y):
        yq = (y + d) % Y
        send(rx.at[x, yq], ry.at[y], ssem.at[E_DY], rsem.at[E_DY], at_y(yq))
    ry[y] = rx[x, y]
    arrived(ry.at[pl.ds(0, Y - 1)], rsem.at[E_DY])
    dy2 = added(ry, Y).astype(BF)

    for v in range(NV):
        for yb in range(Y):
            col = yb * HB + v * HU
            dh = dot(dy2, w2t[:, col:col + HU])
            g1[yb, v] = jnp.where(z1[:, col:col + HU] > 0.0, dh, 0.0).astype(BF)
        for d in (1, 3, 2):
            yq = (y + d) % Y
            send(g1.at[yq, v], gz.at[v, z, y], ssem.at[E_G1], rsem_g.at[v], at_y(yq))
        gz[v, z, y] = g1[y, v]

    def gather_step(v, t):
        if t == 1:
            arrived(gz.at[v, 0, pl.ds(0, Y - 1)], rsem_g.at[v])
        for d in range(2):
            sgn = 1 if d == 0 else -1
            blk = (z - sgn * (t - 1) + Z) % Z
            if t > 1:
                arrived(gz.at[v, 0], rsem_ag.at[v, d, t - 1])
            ref = gz.at[v, blk] if t < half else gz.at[v, blk, pl.ds(d * (Y // 2), Y // 2)]
            send(ref, ref, ssem.at[E_AG], rsem_ag.at[v, d, t], at_z((z + sgn + Z) % Z))

    def product(v):
        for d in range(2):
            arrived(gz.at[v, 0, pl.ds(0, Y // 2)], rsem_ag.at[v, d, half])
        for k in range(Z):
            gt[v, :, k * Y * S:(k + 1) * Y * S] = gz[v, k].reshape(Y * S, HU).T

        def chunk(q, u):
            yb = q * NCH // CB
            off = pl.multiple_of((q % (CB // NCH)) * NCH, NCH)
            dy[v, q // C, q % C] = dot(gt[v], af[yb, :, :, :, pl.ds(off, NCH)].reshape(Z * Y * S, NCH))
            return u

        lax.fori_loop(0, X * C, chunk, 0)
        send(dy.at[v, :, 1 - c], rcy.at[v], ssem.at[E_RC], rsem_c.at[v], partner)

    nxt, prv, opp = (x + 1) % X, (x + X - 1) % X, (x + 2) % X
    hh = HU // 2

    def reduce_core(v):
        arrived(rcy.at[v], rsem_c.at[v])
        for k in range(X):
            rcy[v, k] = rcy[v, k] + dy[v, k, c]
        send(rcy.at[v, opp, pl.ds(0, hh)], rx1.at[v, 0], ssem.at[E_RX], rsem_x.at[v, 0], at_x(nxt))
        send(rcy.at[v, opp, pl.ds(hh, hh)], rx1.at[v, 1], ssem.at[E_RX], rsem_x.at[v, 1], at_x(prv))

    def reduce_x(v):
        arrived(rx1.at[v, 0], rsem_x.at[v, 0])
        rcy[v, nxt, pl.ds(0, hh)] = rcy[v, nxt, pl.ds(0, hh)] + rx1[v, 0]
        send(rcy.at[v, nxt], rx2.at[v, 0], ssem.at[E_RX2], rsem_x.at[v, 2], at_x(nxt))
        arrived(rx1.at[v, 1], rsem_x.at[v, 1])
        rcy[v, prv, pl.ds(hh, hh)] = rcy[v, prv, pl.ds(hh, hh)] + rx1[v, 1]
        send(rcy.at[v, prv], rx2.at[v, 1], ssem.at[E_RX2], rsem_x.at[v, 3], at_x(prv))

    def own_x():
        return jnp.concatenate([xp[m % C, nid * (Y // C) + m // C] for m in range(Y)], axis=0)

    def grad_one(v):
        arrived(rx2.at[v, 0], rsem_x.at[v, 2])
        arrived(rx2.at[v, 1], rsem_x.at[v, 3])
        acc = (rcy[v, x] + rx2[v, 0] + rx2[v, 1]).astype(BF)
        part = dot(acc, own_x())
        if v >= NV // 2:
            part = jnp.concatenate([part[:, LANES // 2:], part[:, 0:LANES // 2]], axis=1)
        per = HU // (Z * 8)
        rows = part.reshape(per, Z, 8, LANES)
        for m in range(per):
            k = (v % (NV // 2)) * per + m
            pb[k] = rows[m] if v < NV // 2 else pb[k] + rows[m]

    def w_begin():
        mark = (lax.broadcasted_iota(jnp.int32, (HB, LANES), 0) == 0) & (lax.broadcasted_iota(jnp.int32, (HB, LANES), 1) == NC)
        for k in range(Y):
            part = lax.dot_general(h1[:, k * HB:(k + 1) * HB], dy2, (((0,), (0,)), ((), ())), preferred_element_type=F32)
            if k == 0:
                part = jnp.where(mark, loss_part, part)
            per = HB // (Y * Z * 8)
            rows = part.reshape(per, Y, Z, 8, LANES)
            for m in range(per):
                q = k * per + m
                wb[q // X, q % X] = rows[m]
        send(wb.at[1 - c], wc, ssem.at[E_WC], rsem.at[E_WC], partner)

    def w_core():
        arrived(wc, rsem.at[E_WC])
        wc[...] = wc[...] + wb[c]
        for d in (1, 3, 2):
            xq = (x + d) % X
            send(wc.at[xq], wx.at[x], ssem.at[E_WX], rsem.at[E_WX], at_x(xq))
        wx[x] = wc[x]

    def w_x():
        arrived(wx.at[pl.ds(0, X - 1)], rsem.at[E_WX])
        wx[x] = added(wx, X)
        for d in (1, 3, 2):
            yq = (y + d) % Y
            send(wx.at[x, yq], wy.at[y], ssem.at[E_WY], rsem.at[E_WY], at_y(yq))
        wy[y] = wx[x, y]

    def w_y():
        arrived(wy.at[pl.ds(0, Y - 1)], rsem.at[E_WY])
        wy[y] = added(wy, Y)
        for d in range(1, Z):
            zq = (z + d) % Z
            send(wy.at[y, zq], wz.at[z], ssem.at[E_WZ], rsem.at[E_WZ], at_z(zq))
        wz[z] = wy[y, z]

    def w_z():
        arrived(wz.at[pl.ds(0, Z - 1)], rsem.at[E_WZ])
        wf[...] = added(wz, Z)
        for d in range(1, Z):
            send(wf, oz.at[z], ssem.at[E_OZ], rsem.at[E_OZ], at_z((z + d) % Z))
        oz[z] = wf[...]

    def o_z():
        arrived(oz.at[pl.ds(0, Z - 1)], rsem.at[E_OZ])
        for d in (1, 3, 2):
            send(oz, oy.at[y], ssem.at[E_OY], rsem.at[E_OY], at_y((y + d) % Y))
        oy[y] = oz[...]

    def o_y():
        arrived(oy.at[pl.ds(0, Y - 1)], rsem.at[E_OY])
        for d in (1, 3, 2):
            send(oy, ox.at[x], ssem.at[E_OX], rsem.at[E_OX], at_x((x + d) % X))
        ox[x] = oy[...]

    def o_x():
        arrived(ox.at[pl.ds(0, X - 1)], rsem.at[E_OX])
        send(ox, oc.at[c], ssem.at[E_OC], rsem.at[E_OC], partner)
        oc[c] = ox[...]

    gather_step(0, 1)
    w_begin()
    for r in range(1, NV + half - 1):
        for v in range(NV):
            t = r - v + 1
            if 1 <= t <= half:
                gather_step(v, t)
        if r == 1:
            w_core()
        if r == half:
            w_x()
            for d in (1, 3):
                for k in range(1, Y):
                    arrived(af.at[0, pl.ds(0, half), 0], rsem_f.at[d // 2, k - 1])
        v = r - half
        if v >= 0:
            product(v)
        if v >= 1:
            reduce_core(v - 1)
        if v >= 2:
            reduce_x(v - 2)
        if r == half + 1:
            w_y()
    product(NV - 1)
    reduce_core(NV - 2)
    reduce_x(NV - 3)
    reduce_core(NV - 1)
    w_z()
    reduce_x(NV - 2)
    for v in range(NV - 2):
        grad_one(v)
    reduce_x(NV - 1)
    o_z()
    grad_one(NV - 2)
    grad_one(NV - 1)

    send(pb, pc, ssem.at[E_PC], rsem.at[E_PC], partner)
    arrived(pc, rsem.at[E_PC])
    pc[...] = pc[...] + pb[...]
    for d in (1, 3, 2):
        xq = (x + d) % X
        send(pc.at[xq], px.at[x], ssem.at[E_PX], rsem.at[E_PX], at_x(xq))
    px[x] = pc[x]
    o_y()
    arrived(px.at[pl.ds(0, X - 1)], rsem.at[E_PX])
    px[x] = added(px, X)
    for d in range(1, Z):
        zq = (z + d) % Z
        send(px.at[x, zq], pz.at[z], ssem.at[E_PZ], rsem.at[E_PZ], at_z(zq))
    pz[z] = px[x, z]
    arrived(pz.at[pl.ds(0, Z - 1)], rsem.at[E_PZ])
    pf[...] = added(pz, Z)
    for d in range(1, Z):
        send(pf, qz.at[z], ssem.at[E_QZ], rsem.at[E_QZ], at_z((z + d) % Z))
    qz[z] = pf[...]
    o_x()
    arrived(qz.at[pl.ds(0, Z - 1)], rsem.at[E_QZ])
    for d in (1, 3, 2):
        send(qz, qy.at[y], ssem.at[E_QY], rsem.at[E_QY], at_y((y + d) % Y))
    qy[y] = qz[...]
    arrived(oc.at[0], rsem.at[E_OC])
    for k in range(C):
        full = oc[k].reshape(H // C, LANES)
        dw2_out[k * (H // C):(k + 1) * (H // C), :] = full[:, 0:NC]
        if k == 0:
            loss_out[...] = jnp.broadcast_to(full[0:1, NC:NC + 1] / count, (8, LANES))
    arrived(qy.at[pl.ds(0, Y - 1)], rsem.at[E_QY])
    for d in (1, 3, 2):
        send(qy, qx.at[x], ssem.at[E_QX], rsem.at[E_QX], at_x((x + d) % X))
    qx[x] = qy[...]
    arrived(qx.at[pl.ds(0, X - 1)], rsem.at[E_QX])
    for yb in range(Y):
        part = qx[:, yb].reshape(HB // 2, LANES).T
        dw1_out[:, yb * HB:yb * HB + HB // 2] = part[0:F]
        dw1_out[:, yb * HB + HB // 2:(yb + 1) * HB] = part[LANES // 2:LANES // 2 + F]

    sent(most(xp), ssem.at[E_X])
    sent(xp.at[0], ssem.at[E_XC])
    sent(af.at[pl.ds(0, Y - 1), :, 0], ssem.at[E_A])
    sent(af.at[pl.ds(0, Y - 1), :, pl.ds(0, 2)], ssem.at[E_B])
    sent(af.at[pl.ds(0, Y - 1), :, 0], ssem.at[E_F])
    sent(sb, ssem.at[E_RING])
    sent(cr.at[pl.ds(0, Z - 1)], ssem.at[E_CNT])
    sent(most(yp), ssem.at[E_Y2])
    sent(yp.at[0], ssem.at[E_Y2C])
    sent(zr.at[pl.ds(0, Z - 1)], ssem.at[E_Z2])
    sent(gr.at[pl.ds(0, Z - 1)], ssem.at[E_G2])
    sent(rc, ssem.at[E_DC])
    sent(rx.at[pl.ds(0, X - 1)], ssem.at[E_DX])
    sent(ry.at[pl.ds(0, Y - 1)], ssem.at[E_DY])
    sent(g1.at[pl.ds(0, Y - 1)], ssem.at[E_G1])
    sent(gz.at[:, pl.ds(0, Z - 1)], ssem.at[E_AG])
    sent(rcy, ssem.at[E_RC])
    sent(rx1, ssem.at[E_RX])
    sent(rx2, ssem.at[E_RX2])
    sent(wc, ssem.at[E_WC])
    sent(wx.at[pl.ds(0, X - 1)], ssem.at[E_WX])
    sent(wy.at[pl.ds(0, Y - 1)], ssem.at[E_WY])
    sent(wz.at[pl.ds(0, Z - 1)], ssem.at[E_WZ])
    sent(oz.at[pl.ds(0, Z - 1)], ssem.at[E_OZ])
    sent(oy.at[pl.ds(0, Y - 1)], ssem.at[E_OY])
    sent(ox.at[pl.ds(0, X - 1)], ssem.at[E_OX])
    sent(oc.at[0], ssem.at[E_OC])
    sent(pc, ssem.at[E_PC])
    sent(px.at[pl.ds(0, X - 1)], ssem.at[E_PX])
    sent(pz.at[pl.ds(0, Z - 1)], ssem.at[E_PZ])
    sent(qz.at[pl.ds(0, Z - 1)], ssem.at[E_QZ])
    sent(qy.at[pl.ds(0, Y - 1)], ssem.at[E_QY])
    sent(qx.at[pl.ds(0, X - 1)], ssem.at[E_QX])


def solution(mesh):
    Y, X, C = Y_DIM, X_DIM, CORES
    Z = mesh.shape["rep"] // Y
    row_spec = P(("rep", "nodes"))

    def device_step(adj_blk, feat_blk, w_one, w_two, label_blk, mask_blk):
        R, S, CB = adj_blk.shape
        F, H = w_one.shape
        NC = w_two.shape[1]
        I = X * C
        NQ = Y * X
        HR = H // (2 * NSUB)
        HB = H // Y
        HU = HB // NV
        NCH = Y * S
        assert R == Z * Y and CB == S * I and F + 2 <= LANES // 2 and NC < LANES
        vm = pltpu.VMEM
        dma = pltpu.SemaphoreType.DMA
        scratch = [
            vm((Y, Z, Y, S, CB), BF),
            vm((LANES, S), F32),
            vm((S, LANES), F32),
            vm((F, H), F32),
            vm((H, NC), F32),
            vm((LANES, H), BF),
            vm((H, LANES), BF),
            vm((LANES, H), BF),
            vm((S, LANES), BF),
            vm((C, NQ, S, LANES), BF),
            vm((Y * CB, H), BF),
            vm((8, LANES), F32),
            vm((Z, 8, LANES), F32),
            vm((2 * NSUB, Z - 1, S, HR), F32),
            vm((2 * NSUB, Z - 1, S, HR), F32),
            vm((S, H), F32),
            vm((S, H), BF),
            vm((S, LANES), BF),
            vm((C, NQ, S, LANES), BF),
            vm((Z, S, LANES), F32),
            vm((Z, S, LANES), F32),
            vm((S, LANES), BF),
            vm((Z, S, LANES), BF),
            vm((Y, X, C, S, LANES), F32),
            vm((Y, X, S, LANES), F32),
            vm((X, Y, S, LANES), F32),
            vm((Y, S, LANES), F32),
            vm((Y, NV, S, HU), BF),
            vm((NV, Z, Y, S, HU), BF),
            vm((NV, HU, Z * Y * S), BF),
            vm((NV, X, C, HU, NCH), F32),
            vm((NV, X, HU, NCH), F32),
            vm((NV, 2, HU // 2, NCH), F32),
            vm((NV, 2, HU, NCH), F32),
            vm((C, X, Y, Z, 8, LANES), F32),
            vm((X, Y, Z, 8, LANES), F32),
            vm((X, Y, Z, 8, LANES), F32),
            vm((Y, Z, 8, LANES), F32),
            vm((Z, 8, LANES), F32),
            vm((8, LANES), F32),
            vm((Z, 8, LANES), F32),
            vm((Y, Z, 8, LANES), F32),
            vm((X, Y, Z, 8, LANES), F32),
            vm((C, X, Y, Z, 8, LANES), F32),
            vm((X, Z, 8, LANES), F32),
            vm((X, Z, 8, LANES), F32),
            vm((X, Z, 8, LANES), F32),
            vm((Z, 8, LANES), F32),
            vm((8, LANES), F32),
            vm((Z, 8, LANES), F32),
            vm((Y, Z, 8, LANES), F32),
            vm((X, Y, Z, 8, LANES), F32),
            dma((NSEM,)),
            dma((NSEM,)),
            dma((Y - 1, Z)),
            dma((2, Y - 1)),
            dma((2, Y - 1)),
            dma((2 * NSUB, Z - 1)),
            dma((NV,)),
            dma((NV, 2, Z // 2 + 1)),
            dma((NV,)),
            dma((NV, 4)),
        ]
        vspec = pl.BlockSpec(memory_space=pltpu.VMEM)
        aspec = pl.BlockSpec(memory_space=pl.ANY)
        dw_one, dw_two, loss = pl.pallas_call(
            functools.partial(_step, (Z, Y, X, C, S, CB, H, F, NC)),
            out_shape=(jax.ShapeDtypeStruct((F, H), F32), jax.ShapeDtypeStruct((H, NC), F32), jax.ShapeDtypeStruct((8, LANES), F32)),
            in_specs=[aspec, vspec, vspec, vspec, aspec, aspec],
            out_specs=(vspec, vspec, vspec),
            scratch_shapes=scratch,
            compiler_params=pltpu.CompilerParams(collective_id=0, has_side_effects=True, vmem_limit_bytes=62 * 1024 * 1024),
            name="gcn_step",
        )(adj_blk.reshape(Z, Y, S, CB), feat_blk.T, label_blk[None, :], mask_blk[None, :], w_one, w_two)
        return loss[0, 0], dw_one, dw_two

    return jax.shard_map(device_step, mesh=mesh, in_specs=(P(None, "nodes", "rep"), row_spec, P(), P(), row_spec, row_spec), out_specs=(P(), P(), P()), check_vma=False)
```

time: 224 us -> 190 us (0.85); the launches traced: 221 us -> 189 us
  Pallas kernels: 206 us -> 183 us
  local copies, waits for them, and re-layouts: 10.9 us -> 5.26 us
  other arithmetic: 2.48 us -> 0 us
    pallas_call x1, Pallas kernels: 206 us -> 183 us  [device_step(): pl.pallas_call(functools.partial(_step, (Z, Y, X, C, S, CB, H, F, NC)), o...]
    unnamed x7 -> x2, local copies, waits for them, and re-layouts: 5.56 us -> 4.08 us
where the time goes in v2:
time: 190 us; the launch traced here: 189 us
  Pallas kernels  183 us (96%)
  local copies, waits for them, and re-layouts  5.26 us (3%)
    pallas_call x1, Pallas kernels, device_step(): pl.pallas_call(functools.partial(_step, (Z, Y, X, C, S, CB, H, F, NC)), o...  183 us
    unnamed x2, local copies, waits for them, and re-layouts  4.08 us

profile of v2, /device:TPU:2, one launch (start us, length us, event | category | flops | bytes accessed | tf_op | source)
XLA Modules:
  0.0 189.4 jit_solution(2037403917107311933)
XLA Ops:
  0.6 183.5 %gcn_step.1 = (f32[50,2048]{1,0:T(8,128)}, f32[2048,121]{1,0:T(8,128)}, f32[8,128]{1,0:T(8,128)}) custom-call(bf16[8,4,64,512]{3,2,1,0:T(8,128)(2,1)} %bitcast.5, bf16[50,64]{1,0:T(8,128)(2,1)} %bitcast.6, s32[1,64]{1,0:T(1,128)} %bitcast.7, s32[1,64]{1,0:T(1,128)} %bitcast.8, f32[50,2048]{1,0:T(8,128)} %w_one.1, f32[2048,121]{1,0:T(8,128)} %w_two.1), custom_call_target="tpu_custom_call" | custom-call | tf_op jit(solution)/shard_map/gcn_step/pallas_call | solution.py:594
  184.1 1.2 slice.3
  185.3 1.8 copy.11
  187.1 2.3 %copy.12 = f32[2048,121]{1,0:T(8,128)} copy(f32[2048,121]{1,0:T(8,128)} %get-tuple-element.14) | data formatting | bytes 1982464

commit v3 on v2

--- a/solution.py
+++ b/solution.py
@@ -13,15 +13,15 @@
 LANES = 128
 NSUB = 2
 NV = 4
-NSEM = 36
+NSEM = 39
 BF = jnp.bfloat16
 F32 = jnp.float32
 
 
 def _step(dims, a_hbm, feat, lab, msk, w_one, w_two, dw1_out, dw2_out, loss_out,
-          af, mt, mtt, w1f, w2f, w1, w2, w2t, xs, xp, y1, cs, cr, sb, rb, z1, h1, y2, yp, zp, zr, g2, gr, dp, rc, rx, ry,
-          g1, gz, gt, dy, rcy, rx1, rx2, wb, wc, wx, wy, wz, wf, oz, oy, ox, oc, pb, pc, px, pz, pf, qz, qy, qx,
-          ssem, rsem, rsem_a, rsem_b, rsem_f, rsem_ring, rsem_g, rsem_ag, rsem_c, rsem_x):
+          af, mt, mtt, w1f, w2f, w1, w2, w2t, xs, xp, y1, cs, cr, sb, rb, z1, h1, y2, yp, zp, zr, g2, gr, dp, rc, rx, ry, ry2, rx2d,
+          d2, dg, ms, mk, gz, gt, dy, rcy, rx1, rx2, wb, wc, wx, wy, wz, wf, oz, oy, ox, oc, pb, pc, px, pz, pf, qz, qy, qx,
+          ssem, rsem, rsem_a, rsem_b, rsem_f, rsem_ring, rsem_ag, rsem_c, rsem_x):
     Z, Y, X, C, S, CB, H, F, NC = dims
     I = X * C
     NQ = Y * X
@@ -75,8 +75,9 @@
             acc = acc + ref[k]
         return acc
 
-    (E_X, E_XC, E_A, E_B, E_F, E_RING, E_CNT, E_Y2, E_Y2C, E_Z2, E_G2, E_DC, E_DX, E_DY, E_G1, E_AG, E_RC, E_RX, E_RX2,
-     E_WC, E_WX, E_WY, E_WZ, E_OZ, E_OY, E_OX, E_OC, E_PC, E_PX, E_PZ, E_QZ, E_QY, E_QX, E_LA, E_L1, E_L2) = range(NSEM)
+    (E_X, E_XC, E_A, E_B, E_F, E_RING, E_CNT, E_Y2, E_Y2C, E_Z2, E_G2, E_DC, E_DX, E_DY, E_AG, E_RC, E_RX, E_RX2,
+     E_WC, E_WX, E_WY, E_WZ, E_OZ, E_OY, E_OX, E_OC, E_PC, E_PX, E_PZ, E_QZ, E_QY, E_QX, E_LA, E_L1, E_L2,
+     E_M, E_DY2, E_DX2, E_DG) = range(NSEM)
 
     load_a = pltpu.make_async_copy(a_hbm, af.at[y], ssem.at[E_LA])
     load_1 = pltpu.make_async_copy(w_one, w1f, ssem.at[E_L1])
@@ -124,11 +125,25 @@
         for d in (1, 3, 2):
             yq = (y + d) % Y
             send(af.at[y, zc, yq], af.at[y, zc, yq], ssem.at[E_A], rsem_a.at[d - 1, zc], at_y(yq))
-    for d in (1, 3):
-        yq = (y + d) % Y
-        for k in range(1, Y):
+    def spread_a(k):
+        for d in (1, 3):
+            yq = (y + d) % Y
             ya = (yq + k) % Y
             send(af.at[y, :, ya], af.at[y, :, ya], ssem.at[E_B], rsem_b.at[d // 2, k - 1], at_y(yq))
+
+    def forward_a():
+        for k in range(1, Y):
+            for d in (1, 3):
+                arrived(af.at[0, :, 0], rsem_b.at[d // 2, k - 1])
+        for k in range(1, Y):
+            for d in (1, 3):
+                ys, yq = (y - d + Y) % Y, (y + d) % Y
+                lo = 0 if d == 1 else half
+                ya = (yq + k) % Y
+                send(af.at[ys, pl.ds(lo, half), ya], af.at[ys, pl.ds(lo, half), ya], ssem.at[E_F], rsem_f.at[d // 2, k - 1], at_y(yq))
+
+    spread_a(1)
+    spread_a(2)
 
     load_1.wait()
     w1[...] = jnp.zeros_like(w1)
@@ -208,21 +223,19 @@
     send(yp.at[c], yp.at[c], ssem.at[E_Y2C], rsem.at[E_Y2C], partner)
     arrived(yp.at[0], rsem.at[E_Y2C])
     for yb in range(Y):
+        ms[yb] = jnp.where(z1[:, yb * HB:(yb + 1) * HB] > 0.0, 1.0, 0.0).astype(BF)
+    for yb in range(Y):
         part = dot(af[yb, :, y].reshape(Z * S, CB), plane_rows(yp, yb)).reshape(Z, S, LANES)
         zp[...] = part if yb == 0 else zp[...] + part
     for d in range(1, Z):
         zq = (z + d) % Z
         send(zp.at[zq], zr.at[z], ssem.at[E_Z2], rsem.at[E_Z2], at_z(zq))
     zr[z] = zp[z]
-    for d in (1, 3):
-        for k in range(1, Y):
-            arrived(af.at[0, :, 0], rsem_b.at[d // 2, k - 1])
-    for d in (1, 3):
-        ys, yq = (y - d + Y) % Y, (y + d) % Y
-        lo = 0 if d == 1 else half
-        for k in range(1, Y):
-            ya = (yq + k) % Y
-            send(af.at[ys, pl.ds(lo, half), ya], af.at[ys, pl.ds(lo, half), ya], ssem.at[E_F], rsem_f.at[d // 2, k - 1], at_y(yq))
+    for d in (1, 3, 2):
+        yq = (y + d) % Y
+        send(ms.at[yq], mk.at[y], ssem.at[E_M], rsem.at[E_M], at_y(yq))
+    mk[y] = ms[y]
+    spread_a(3)
     arrived(zr.at[pl.ds(0, Z - 1)], rsem.at[E_Z2])
     z2 = added(zr, Z)
 
@@ -252,32 +265,42 @@
     send(dp.at[:, :, 1 - c], rc, ssem.at[E_DC], rsem.at[E_DC], partner)
     arrived(rc, rsem.at[E_DC])
     rc[...] = rc[...] + dp[:, :, c]
-    for d in range(1, X):
-        xq = (x + d) % X
-        send(rc.at[:, xq], rx.at[x], ssem.at[E_DX], rsem.at[E_DX], at_x(xq))
-    rx[x] = rc[:, x]
+    sh = S // 2
+    for d in (1, 3, 2):
+        xq, yq = (x + d) % X, (y + d) % Y
+        send(rc.at[:, xq, pl.ds(0, sh)], rx.at[x], ssem.at[E_DX], rsem.at[E_DX], at_x(xq))
+        send(rc.at[yq, :, pl.ds(sh, sh)], ry.at[y], ssem.at[E_DY], rsem.at[E_DY], at_y(yq))
+    rx[x] = rc[:, x, 0:sh]
+    ry[y] = rc[y, :, sh:S]
     arrived(rx.at[pl.ds(0, X - 1)], rsem.at[E_DX])
     rx[x] = added(rx, X)
-    for d in range(1, Y):
+    for d in (1, 3, 2):
         yq = (y + d) % Y
-        send(rx.at[x, yq], ry.at[y], ssem.at[E_DY], rsem.at[E_DY], at_y(yq))
-    ry[y] = rx[x, y]
+        send(rx.at[x, yq], ry2.at[y], ssem.at[E_DY2], rsem.at[E_DY2], at_y(yq))
+    ry2[y] = rx[x, y]
     arrived(ry.at[pl.ds(0, Y - 1)], rsem.at[E_DY])
-    dy2 = added(ry, Y).astype(BF)
-
-    for v in range(NV):
-        for yb in range(Y):
-            col = yb * HB + v * HU
-            dh = dot(dy2, w2t[:, col:col + HU])
-            g1[yb, v] = jnp.where(z1[:, col:col + HU] > 0.0, dh, 0.0).astype(BF)
-        for d in (1, 3, 2):
-            yq = (y + d) % Y
-            send(g1.at[yq, v], gz.at[v, z, y], ssem.at[E_G1], rsem_g.at[v], at_y(yq))
-        gz[v, z, y] = g1[y, v]
+    ry[y] = added(ry, Y)
+    for d in (1, 3, 2):
+        xq = (x + d) % X
+        send(ry.at[y, xq], rx2d.at[x], ssem.at[E_DX2], rsem.at[E_DX2], at_x(xq))
+    rx2d[x] = ry[y, x]
+    arrived(ry2.at[pl.ds(0, Y - 1)], rsem.at[E_DY2])
+    arrived(rx2d.at[pl.ds(0, X - 1)], rsem.at[E_DX2])
+    d2[0:sh] = added(ry2, Y).astype(BF)
+    d2[sh:S] = added(rx2d, X).astype(BF)
+    for d in (1, 3, 2):
+        send(d2, dg.at[y], ssem.at[E_DG], rsem.at[E_DG], at_y((y + d) % Y))
+    dg[y] = d2[...]
+    forward_a()
+    dy2 = d2[...]
+
+    def g_one(v):
+        col = pl.multiple_of(y * HB + v * HU, HU)
+        dh = dot(dg[...].reshape(Y * S, LANES), w2t[:, pl.ds(col, HU)])
+        keep = mk[:, :, v * HU:(v + 1) * HU].reshape(Y * S, HU).astype(F32)
+        gz[v, z] = jnp.where(keep > 0.0, dh, 0.0).astype(BF).reshape(Y, S, HU)
 
     def gather_step(v, t):
-        if t == 1:
-            arrived(gz.at[v, 0, pl.ds(0, Y - 1)], rsem_g.at[v])
         for d in range(2):
             sgn = 1 if d == 0 else -1
             blk = (z - sgn * (t - 1) + Z) % Z
@@ -292,13 +315,21 @@
         for k in range(Z):
             gt[v, :, k * Y * S:(k + 1) * Y * S] = gz[v, k].reshape(Y * S, HU).T
 
-        def chunk(q, u):
-            yb = q * NCH // CB
+        def chunk(k, u):
+            hops = k // (CB // NCH)
+            yb = lax.rem(y + hops + jnp.where(hops == 2, 1, 0) - jnp.where(hops == 3, 1, 0), Y)
+            q = yb * (CB // NCH) + k % (CB // NCH)
             off = pl.multiple_of((q % (CB // NCH)) * NCH, NCH)
             dy[v, q // C, q % C] = dot(gt[v], af[yb, :, :, :, pl.ds(off, NCH)].reshape(Z * Y * S, NCH))
             return u
 
-        lax.fori_loop(0, X * C, chunk, 0)
+        first = (Y - 1) * (CB // NCH) if v == 0 else 0
+        lax.fori_loop(0, first, chunk, 0)
+        if v == 0:
+            for d in (1, 3):
+                for k in range(1, Y):
+                    arrived(af.at[0, pl.ds(0, half), 0], rsem_f.at[d // 2, k - 1])
+        lax.fori_loop(first, X * C, chunk, 0)
         send(dy.at[v, :, 1 - c], rcy.at[v], ssem.at[E_RC], rsem_c.at[v], partner)
 
     nxt, prv, opp = (x + 1) % X, (x + X - 1) % X, (x + 2) % X
@@ -396,41 +427,23 @@
         send(ox, oc.at[c], ssem.at[E_OC], rsem.at[E_OC], partner)
         oc[c] = ox[...]
 
-    gather_step(0, 1)
-    w_begin()
-    for r in range(1, NV + half - 1):
-        for v in range(NV):
-            t = r - v + 1
-            if 1 <= t <= half:
-                gather_step(v, t)
-        if r == 1:
-            w_core()
-        if r == half:
-            w_x()
-            for d in (1, 3):
-                for k in range(1, Y):
-                    arrived(af.at[0, pl.ds(0, half), 0], rsem_f.at[d // 2, k - 1])
-        v = r - half
-        if v >= 0:
-            product(v)
-        if v >= 1:
-            reduce_core(v - 1)
-        if v >= 2:
-            reduce_x(v - 2)
-        if r == half + 1:
-            w_y()
-    product(NV - 1)
-    reduce_core(NV - 2)
-    reduce_x(NV - 3)
-    reduce_core(NV - 1)
-    w_z()
-    reduce_x(NV - 2)
-    for v in range(NV - 2):
-        grad_one(v)
-    reduce_x(NV - 1)
-    o_z()
-    grad_one(NV - 2)
-    grad_one(NV - 1)
+    arrived(mk.at[pl.ds(0, Y - 1)], rsem.at[E_M])
+    arrived(dg.at[pl.ds(0, Y - 1)], rsem.at[E_DG])
+    steps = [
+        (g_one, 0), (gather_step, 0, 1), (g_one, 1), (gather_step, 1, 1), (g_one, 2), (g_one, 3), (w_begin,),
+        (gather_step, 0, 2), (gather_step, 1, 2), (w_core,)]
+    for t in range(3, half + 1):
+        steps += [(gather_step, 0, t), (gather_step, 1, t)]
+    steps += [(gather_step, 2, 1), (gather_step, 3, 1), (product, 0), (gather_step, 2, 2), (gather_step, 3, 2), (w_x,), (product, 1),
+              (reduce_core, 0)]
+    for t in range(3, half + 1):
+        steps += [(gather_step, 2, t), (gather_step, 3, t)]
+        if t == 3:
+            steps += [(reduce_core, 1), (reduce_x, 0), (w_y,)]
+    steps += [(reduce_x, 1), (product, 2), (product, 3), (reduce_core, 2), (grad_one, 0), (reduce_core, 3), (reduce_x, 2), (w_z,),
+              (grad_one, 1), (reduce_x, 3), (o_z,), (grad_one, 2), (grad_one, 3)]
+    for step in steps:
+        step[0](*step[1:])
 
     send(pb, pc, ssem.at[E_PC], rsem.at[E_PC], partner)
     arrived(pc, rsem.at[E_PC])
@@ -486,7 +499,10 @@
     sent(rc, ssem.at[E_DC])
     sent(rx.at[pl.ds(0, X - 1)], ssem.at[E_DX])
     sent(ry.at[pl.ds(0, Y - 1)], ssem.at[E_DY])
-    sent(g1.at[pl.ds(0, Y - 1)], ssem.at[E_G1])
+    sent(ry2.at[pl.ds(0, Y - 1)], ssem.at[E_DY2])
+    sent(rx2d.at[pl.ds(0, X - 1)], ssem.at[E_DX2])
+    sent(dg.at[pl.ds(0, Y - 1)], ssem.at[E_DG])
+    sent(mk.at[pl.ds(0, Y - 1)], ssem.at[E_M])
     sent(gz.at[:, pl.ds(0, Z - 1)], ssem.at[E_AG])
     sent(rcy, ssem.at[E_RC])
     sent(rx1, ssem.at[E_RX])
@@ -551,9 +567,14 @@
             vm((Z, S, LANES), BF),
             vm((Y, X, C, S, LANES), F32),
             vm((Y, X, S, LANES), F32),
-            vm((X, Y, S, LANES), F32),
-            vm((Y, S, LANES), F32),
-            vm((Y, NV, S, HU), BF),
+            vm((X, Y, S // 2, LANES), F32),
+            vm((Y, X, S // 2, LANES), F32),
+            vm((Y, S // 2, LANES), F32),
+            vm((X, S // 2, LANES), F32),
+            vm((S, LANES), BF),
+            vm((Y, S, LANES), BF),
+            vm((Y, S, HB), BF),
+            vm((Y, S, HB), BF),
             vm((NV, Z, Y, S, HU), BF),
             vm((NV, HU, Z * Y * S), BF),
             vm((NV, X, C, HU, NCH), F32),
@@ -584,7 +605,6 @@
             dma((2, Y - 1)),
             dma((2, Y - 1)),
             dma((2 * NSUB, Z - 1)),
-            dma((NV,)),
             dma((NV, 2, Z // 2 + 1)),
             dma((NV,)),
             dma((NV, 4)),

time: 190 us -> 183 us (0.963)
  Pallas kernels: 183 us -> 177 us
    pallas_call x1, Pallas kernels: 183 us -> 177 us  [device_step(): pl.pallas_call(functools.partial(_step, (Z, Y, X, C, S, CB, H, F, NC)), o...]
where the time goes in v3:
time: 183 us
  Pallas kernels  177 us (97%)
  local copies, waits for them, and re-layouts  5.26 us (3%)
    pallas_call x1, Pallas kernels, device_step(): pl.pallas_call(functools.partial(_step, (Z, Y, X, C, S, CB, H, F, NC)), o...  177 us
    unnamed x2, local copies, waits for them, and re-layouts  4.08 us

profile of v3, /device:TPU:2, one launch (start us, length us, event | category | flops | bytes accessed | tf_op | source)
XLA Modules:
  0.0 182.9 jit_solution(18254948150815954795)
XLA Ops:
  0.6 177.0 %gcn_step.1 = (f32[50,2048]{1,0:T(8,128)}, f32[2048,121]{1,0:T(8,128)}, f32[8,128]{1,0:T(8,128)}) custom-call(bf16[8,4,64,512]{3,2,1,0:T(8,128)(2,1)} %bitcast.5, bf16[50,64]{1,0:T(8,128)(2,1)} %bitcast.6, s32[1,64]{1,0:T(1,128)} %bitcast.7, s32[1,64]{1,0:T(1,128)} %bitcast.8, f32[50,2048]{1,0:T(8,128)} %w_one.1, f32[2048,121]{1,0:T(8,128)} %w_two.1), custom_call_target="tpu_custom_call" | custom-call | tf_op jit(solution)/shard_map/gcn_step/pallas_call | solution.py:614
  177.7 1.2 slice.3
  178.9 1.8 copy.11
  180.7 2.3 %copy.12 = f32[2048,121]{1,0:T(8,128)} copy(f32[2048,121]{1,0:T(8,128)} %get-tuple-element.14) | data formatting | bytes 1982464

commit v4 on v3

--- a/solution.py
+++ b/solution.py
@@ -11,16 +11,16 @@
 X_DIM = 4
 CORES = 2
 LANES = 128
-NSUB = 2
+NSUB = 4
 NV = 4
-NSEM = 39
+NSEM = 41
 BF = jnp.bfloat16
 F32 = jnp.float32
 
 
 def _step(dims, a_hbm, feat, lab, msk, w_one, w_two, dw1_out, dw2_out, loss_out,
           af, mt, mtt, w1f, w2f, w1, w2, w2t, xs, xp, y1, cs, cr, sb, rb, z1, h1, y2, yp, zp, zr, g2, gr, dp, rc, rx, ry, ry2, rx2d,
-          d2, dg, ms, mk, gz, gt, dy, rcy, rx1, rx2, wb, wc, wx, wy, wz, wf, oz, oy, ox, oc, pb, pc, px, pz, pf, qz, qy, qx,
+          d2, dg, ms, mk, gz, gt, dy, rcy, rx1, rx2, wb, wc, wx, wy, wz, wf, oz, oy, ox, oc, pb, pc, px, pz, pf, qz, qy, qx, qxy, qyx,
           ssem, rsem, rsem_a, rsem_b, rsem_f, rsem_ring, rsem_ag, rsem_c, rsem_x):
     Z, Y, X, C, S, CB, H, F, NC = dims
     I = X * C
@@ -36,6 +36,8 @@
     chip = y * X + x
     partner = (rid, x * C + 1 - c)
 
+    far = sorted(range(1, Z), key=lambda d: -min(d, Z - d))
+
     def at_z(zz):
         return (zz * Y + y, nid)
 
@@ -77,7 +79,7 @@
 
     (E_X, E_XC, E_A, E_B, E_F, E_RING, E_CNT, E_Y2, E_Y2C, E_Z2, E_G2, E_DC, E_DX, E_DY, E_AG, E_RC, E_RX, E_RX2,
      E_WC, E_WX, E_WY, E_WZ, E_OZ, E_OY, E_OX, E_OC, E_PC, E_PX, E_PZ, E_QZ, E_QY, E_QX, E_LA, E_L1, E_L2,
-     E_M, E_DY2, E_DX2, E_DG) = range(NSEM)
+     E_M, E_DY2, E_DX2, E_DG, E_QXY, E_QYX) = range(NSEM)
 
     load_a = pltpu.make_async_copy(a_hbm, af.at[y], ssem.at[E_LA])
     load_1 = pltpu.make_async_copy(w_one, w1f, ssem.at[E_L1])
@@ -87,7 +89,7 @@
     load_2.start()
 
     bar = pltpu.get_barrier_semaphore()
-    for d in range(1, Z):
+    for d in far:
         pl.semaphore_signal(bar, inc=1, device_id=at_z((z + d) % Z), device_id_type=pl.DeviceIdType.MESH)
 
     def greet_plane(d, u):
@@ -122,7 +124,7 @@
     order.append(0)
     for k in order:
         zc = (z + k + Z) % Z
-        for d in (1, 3, 2):
+        for d in (2, 1, 3):
             yq = (y + d) % Y
             send(af.at[y, zc, yq], af.at[y, zc, yq], ssem.at[E_A], rsem_a.at[d - 1, zc], at_y(yq))
     def spread_a(k):
@@ -165,11 +167,11 @@
 
     def ring(t, u):
         s, j = t // (2 * NSUB), t % (2 * NSUB)
-        up = j < NSUB
+        up = j % 2 == 0
         dest = lax.rem(jnp.where(up, z - 1 - s, z + 1 + s) + 2 * Z, Z)
         nb = lax.rem(jnp.where(up, z + 1, z - 1) + Z, Z)
         col = pl.multiple_of(j * HR, HR)
-        fresh = ((j == 0) & ((s < half) | (s == Z - 1))) | ((j == NSUB) & (s < half - 1))
+        fresh = ((j == 0) & ((s < half) | (s == Z - 1))) | ((j == 1) & (s < half - 1))
 
         @pl.when(s == 0)
         def _():
@@ -217,7 +219,7 @@
     counted = jnp.sum(jnp.where(lane[0:1] == F, counted, 0.0), axis=1, keepdims=True)
     cs[...] = jnp.broadcast_to(counted, (8, LANES))
     cr[z] = cs[...]
-    for d in range(1, Z):
+    for d in far:
         send(cs, cr.at[z], ssem.at[E_CNT], rsem.at[E_CNT], at_z((z + d) % Z))
     arrived(most(yp), rsem.at[E_Y2])
     send(yp.at[c], yp.at[c], ssem.at[E_Y2C], rsem.at[E_Y2C], partner)
@@ -227,11 +229,11 @@
     for yb in range(Y):
         part = dot(af[yb, :, y].reshape(Z * S, CB), plane_rows(yp, yb)).reshape(Z, S, LANES)
         zp[...] = part if yb == 0 else zp[...] + part
-    for d in range(1, Z):
+    for d in far:
         zq = (z + d) % Z
         send(zp.at[zq], zr.at[z], ssem.at[E_Z2], rsem.at[E_Z2], at_z(zq))
     zr[z] = zp[z]
-    for d in (1, 3, 2):
+    for d in (2, 1, 3):
         yq = (y + d) % Y
         send(ms.at[yq], mk.at[y], ssem.at[E_M], rsem.at[E_M], at_y(yq))
     mk[y] = ms[y]
@@ -253,7 +255,7 @@
     loss_part = -jnp.sum(weights * picked, axis=0, keepdims=True)
     diff = jnp.where(real, jnp.exp(log_probs), 0.0) - hot.astype(F32)
     g2[...] = (diff * (weights / count)).astype(BF)
-    for d in range(1, Z):
+    for d in far:
         send(g2, gr.at[z], ssem.at[E_G2], rsem.at[E_G2], at_z((z + d) % Z))
     gr[z] = g2[...]
     arrived(gr.at[pl.ds(0, Z - 1)], rsem.at[E_G2])
@@ -266,7 +268,7 @@
     arrived(rc, rsem.at[E_DC])
     rc[...] = rc[...] + dp[:, :, c]
     sh = S // 2
-    for d in (1, 3, 2):
+    for d in (2, 1, 3):
         xq, yq = (x + d) % X, (y + d) % Y
         send(rc.at[:, xq, pl.ds(0, sh)], rx.at[x], ssem.at[E_DX], rsem.at[E_DX], at_x(xq))
         send(rc.at[yq, :, pl.ds(sh, sh)], ry.at[y], ssem.at[E_DY], rsem.at[E_DY], at_y(yq))
@@ -274,13 +276,13 @@
     ry[y] = rc[y, :, sh:S]
     arrived(rx.at[pl.ds(0, X - 1)], rsem.at[E_DX])
     rx[x] = added(rx, X)
-    for d in (1, 3, 2):
+    for d in (2, 1, 3):
         yq = (y + d) % Y
         send(rx.at[x, yq], ry2.at[y], ssem.at[E_DY2], rsem.at[E_DY2], at_y(yq))
     ry2[y] = rx[x, y]
     arrived(ry.at[pl.ds(0, Y - 1)], rsem.at[E_DY])
     ry[y] = added(ry, Y)
-    for d in (1, 3, 2):
+    for d in (2, 1, 3):
         xq = (x + d) % X
         send(ry.at[y, xq], rx2d.at[x], ssem.at[E_DX2], rsem.at[E_DX2], at_x(xq))
     rx2d[x] = ry[y, x]
@@ -288,7 +290,7 @@
     arrived(rx2d.at[pl.ds(0, X - 1)], rsem.at[E_DX2])
     d2[0:sh] = added(ry2, Y).astype(BF)
     d2[sh:S] = added(rx2d, X).astype(BF)
-    for d in (1, 3, 2):
+    for d in (2, 1, 3):
         send(d2, dg.at[y], ssem.at[E_DG], rsem.at[E_DG], at_y((y + d) % Y))
     dg[y] = d2[...]
     forward_a()
@@ -309,46 +311,61 @@
             ref = gz.at[v, blk] if t < half else gz.at[v, blk, pl.ds(d * (Y // 2), Y // 2)]
             send(ref, ref, ssem.at[E_AG], rsem_ag.at[v, d, t], at_z((z + sgn + Z) % Z))
 
-    def product(v):
-        for d in range(2):
-            arrived(gz.at[v, 0, pl.ds(0, Y // 2)], rsem_ag.at[v, d, half])
-        for k in range(Z):
-            gt[v, :, k * Y * S:(k + 1) * Y * S] = gz[v, k].reshape(Y * S, HU).T
-
-        def chunk(k, u):
-            hops = k // (CB // NCH)
-            yb = lax.rem(y + hops + jnp.where(hops == 2, 1, 0) - jnp.where(hops == 3, 1, 0), Y)
-            q = yb * (CB // NCH) + k % (CB // NCH)
-            off = pl.multiple_of((q % (CB // NCH)) * NCH, NCH)
-            dy[v, q // C, q % C] = dot(gt[v], af[yb, :, :, :, pl.ds(off, NCH)].reshape(Z * Y * S, NCH))
-            return u
-
-        first = (Y - 1) * (CB // NCH) if v == 0 else 0
-        lax.fori_loop(0, first, chunk, 0)
-        if v == 0:
+    def piece(v):
+        return pl.ds(v % 2 * HU, HU)
+
+    def product(p):
+        for v in (2 * p, 2 * p + 1):
+            for d in range(2):
+                arrived(gz.at[v, 0, pl.ds(0, Y // 2)], rsem_ag.at[v, d, half])
+            for k in range(Z):
+                gt[p, piece(v), k * Y * S:(k + 1) * Y * S] = gz[v, k].reshape(Y * S, HU).T
+
+        def chunk(core):
+            def body(k, u):
+                yb = lax.rem(y + k + jnp.where(k == 2, 1, 0) - jnp.where(k == 3, 1, 0), Y)
+                q = yb * C + core
+                off = pl.multiple_of(core * NCH, NCH)
+                dy[p, q // C, core] = dot(gt[p], af[yb, :, :, :, pl.ds(off, NCH)].reshape(Z * Y * S, NCH))
+                return u
+            return body
+
+        first = Y - 1 if p == 0 else 0
+        lax.fori_loop(0, first, chunk(1 - c), 0)
+        if p == 0:
             for d in (1, 3):
                 for k in range(1, Y):
                     arrived(af.at[0, pl.ds(0, half), 0], rsem_f.at[d // 2, k - 1])
-        lax.fori_loop(first, X * C, chunk, 0)
-        send(dy.at[v, :, 1 - c], rcy.at[v], ssem.at[E_RC], rsem_c.at[v], partner)
+        lax.fori_loop(first, Y, chunk(1 - c), 0)
+        for v in (2 * p, 2 * p + 1):
+            send(dy.at[p, :, 1 - c, piece(v)], rcy.at[p, :, piece(v)], ssem.at[E_RC], rsem_c.at[v], partner)
+        lax.fori_loop(0, Y, chunk(c), 0)
 
     nxt, prv, opp = (x + 1) % X, (x + X - 1) % X, (x + 2) % X
     hh = HU // 2
 
+    def low(v):
+        return pl.ds(v % 2 * HU, hh)
+
+    def high(v):
+        return pl.ds(v % 2 * HU + hh, hh)
+
     def reduce_core(v):
-        arrived(rcy.at[v], rsem_c.at[v])
+        p = v // 2
+        arrived(rcy.at[p, :, piece(v)], rsem_c.at[v])
         for k in range(X):
-            rcy[v, k] = rcy[v, k] + dy[v, k, c]
-        send(rcy.at[v, opp, pl.ds(0, hh)], rx1.at[v, 0], ssem.at[E_RX], rsem_x.at[v, 0], at_x(nxt))
-        send(rcy.at[v, opp, pl.ds(hh, hh)], rx1.at[v, 1], ssem.at[E_RX], rsem_x.at[v, 1], at_x(prv))
+            rcy[p, k, piece(v)] = rcy[p, k, piece(v)] + dy[p, k, c, piece(v)]
+        send(rcy.at[p, opp, low(v)], rx1.at[v, 0], ssem.at[E_RX], rsem_x.at[v, 0], at_x(nxt))
+        send(rcy.at[p, opp, high(v)], rx1.at[v, 1], ssem.at[E_RX], rsem_x.at[v, 1], at_x(prv))
 
     def reduce_x(v):
+        p = v // 2
         arrived(rx1.at[v, 0], rsem_x.at[v, 0])
-        rcy[v, nxt, pl.ds(0, hh)] = rcy[v, nxt, pl.ds(0, hh)] + rx1[v, 0]
-        send(rcy.at[v, nxt], rx2.at[v, 0], ssem.at[E_RX2], rsem_x.at[v, 2], at_x(nxt))
+        rcy[p, nxt, low(v)] = rcy[p, nxt, low(v)] + rx1[v, 0]
+        send(rcy.at[p, nxt, piece(v)], rx2.at[v, 0], ssem.at[E_RX2], rsem_x.at[v, 2], at_x(nxt))
         arrived(rx1.at[v, 1], rsem_x.at[v, 1])
-        rcy[v, prv, pl.ds(hh, hh)] = rcy[v, prv, pl.ds(hh, hh)] + rx1[v, 1]
-        send(rcy.at[v, prv], rx2.at[v, 1], ssem.at[E_RX2], rsem_x.at[v, 3], at_x(prv))
+        rcy[p, prv, high(v)] = rcy[p, prv, high(v)] + rx1[v, 1]
+        send(rcy.at[p, prv, piece(v)], rx2.at[v, 1], ssem.at[E_RX2], rsem_x.at[v, 3], at_x(prv))
 
     def own_x():
         return jnp.concatenate([xp[m % C, nid * (Y // C) + m // C] for m in range(Y)], axis=0)
@@ -356,7 +373,7 @@
     def grad_one(v):
         arrived(rx2.at[v, 0], rsem_x.at[v, 2])
         arrived(rx2.at[v, 1], rsem_x.at[v, 3])
-        acc = (rcy[v, x] + rx2[v, 0] + rx2[v, 1]).astype(BF)
+        acc = (rcy[v // 2, x, piece(v)] + rx2[v, 0] + rx2[v, 1]).astype(BF)
         part = dot(acc, own_x())
         if v >= NV // 2:
             part = jnp.concatenate([part[:, LANES // 2:], part[:, 0:LANES // 2]], axis=1)
@@ -382,7 +399,7 @@
     def w_core():
         arrived(wc, rsem.at[E_WC])
         wc[...] = wc[...] + wb[c]
-        for d in (1, 3, 2):
+        for d in (2, 1, 3):
             xq = (x + d) % X
             send(wc.at[xq], wx.at[x], ssem.at[E_WX], rsem.at[E_WX], at_x(xq))
         wx[x] = wc[x]
@@ -390,7 +407,7 @@
     def w_x():
         arrived(wx.at[pl.ds(0, X - 1)], rsem.at[E_WX])
         wx[x] = added(wx, X)
-        for d in (1, 3, 2):
+        for d in (2, 1, 3):
             yq = (y + d) % Y
             send(wx.at[x, yq], wy.at[y], ssem.at[E_WY], rsem.at[E_WY], at_y(yq))
         wy[y] = wx[x, y]
@@ -398,7 +415,7 @@
     def w_y():
         arrived(wy.at[pl.ds(0, Y - 1)], rsem.at[E_WY])
         wy[y] = added(wy, Y)
-        for d in range(1, Z):
+        for d in far:
             zq = (z + d) % Z
             send(wy.at[y, zq], wz.at[z], ssem.at[E_WZ], rsem.at[E_WZ], at_z(zq))
         wz[z] = wy[y, z]
@@ -406,19 +423,19 @@
     def w_z():
         arrived(wz.at[pl.ds(0, Z - 1)], rsem.at[E_WZ])
         wf[...] = added(wz, Z)
-        for d in range(1, Z):
+        for d in far:
             send(wf, oz.at[z], ssem.at[E_OZ], rsem.at[E_OZ], at_z((z + d) % Z))
         oz[z] = wf[...]
 
     def o_z():
         arrived(oz.at[pl.ds(0, Z - 1)], rsem.at[E_OZ])
-        for d in (1, 3, 2):
+        for d in (2, 1, 3):
             send(oz, oy.at[y], ssem.at[E_OY], rsem.at[E_OY], at_y((y + d) % Y))
         oy[y] = oz[...]
 
     def o_y():
         arrived(oy.at[pl.ds(0, Y - 1)], rsem.at[E_OY])
-        for d in (1, 3, 2):
+        for d in (2, 1, 3):
             send(oy, ox.at[x], ssem.at[E_OX], rsem.at[E_OX], at_x((x + d) % X))
         ox[x] = oy[...]
 
@@ -434,41 +451,44 @@
         (gather_step, 0, 2), (gather_step, 1, 2), (w_core,)]
     for t in range(3, half + 1):
         steps += [(gather_step, 0, t), (gather_step, 1, t)]
-    steps += [(gather_step, 2, 1), (gather_step, 3, 1), (product, 0), (gather_step, 2, 2), (gather_step, 3, 2), (w_x,), (product, 1),
-              (reduce_core, 0)]
+    steps += [(gather_step, 2, 1), (gather_step, 3, 1), (product, 0), (gather_step, 2, 2), (gather_step, 3, 2), (w_x,), (reduce_core, 0),
+              (reduce_core, 1)]
     for t in range(3, half + 1):
         steps += [(gather_step, 2, t), (gather_step, 3, t)]
         if t == 3:
-            steps += [(reduce_core, 1), (reduce_x, 0), (w_y,)]
-    steps += [(reduce_x, 1), (product, 2), (product, 3), (reduce_core, 2), (grad_one, 0), (reduce_core, 3), (reduce_x, 2), (w_z,),
-              (grad_one, 1), (reduce_x, 3), (o_z,), (grad_one, 2), (grad_one, 3)]
+            steps += [(reduce_x, 0), (w_y,), (reduce_x, 1)]
+    steps += [(product, 1), (reduce_core, 2), (reduce_core, 3), (grad_one, 0), (grad_one, 1), (reduce_x, 2), (reduce_x, 3), (w_z,),
+              (o_z,), (grad_one, 2), (grad_one, 3)]
     for step in steps:
         step[0](*step[1:])
 
     send(pb, pc, ssem.at[E_PC], rsem.at[E_PC], partner)
     arrived(pc, rsem.at[E_PC])
     pc[...] = pc[...] + pb[...]
-    for d in (1, 3, 2):
+    for d in (2, 1, 3):
         xq = (x + d) % X
         send(pc.at[xq], px.at[x], ssem.at[E_PX], rsem.at[E_PX], at_x(xq))
     px[x] = pc[x]
     o_y()
     arrived(px.at[pl.ds(0, X - 1)], rsem.at[E_PX])
     px[x] = added(px, X)
-    for d in range(1, Z):
+    for d in far:
         zq = (z + d) % Z
         send(px.at[x, zq], pz.at[z], ssem.at[E_PZ], rsem.at[E_PZ], at_z(zq))
     pz[z] = px[x, z]
     arrived(pz.at[pl.ds(0, Z - 1)], rsem.at[E_PZ])
     pf[...] = added(pz, Z)
-    for d in range(1, Z):
+    for d in far:
         send(pf, qz.at[z], ssem.at[E_QZ], rsem.at[E_QZ], at_z((z + d) % Z))
     qz[z] = pf[...]
     o_x()
     arrived(qz.at[pl.ds(0, Z - 1)], rsem.at[E_QZ])
-    for d in (1, 3, 2):
-        send(qz, qy.at[y], ssem.at[E_QY], rsem.at[E_QY], at_y((y + d) % Y))
-    qy[y] = qz[...]
+    zl, zh = pl.ds(0, half), pl.ds(half, half)
+    for d in (2, 1, 3):
+        send(qz.at[zl], qy.at[y], ssem.at[E_QY], rsem.at[E_QY], at_y((y + d) % Y))
+        send(qz.at[zh], qx.at[x], ssem.at[E_QX], rsem.at[E_QX], at_x((x + d) % X))
+    qy[y] = qz[zl]
+    qx[x] = qz[zh]
     arrived(oc.at[0], rsem.at[E_OC])
     for k in range(C):
         full = oc[k].reshape(H // C, LANES)
@@ -476,12 +496,17 @@
         if k == 0:
             loss_out[...] = jnp.broadcast_to(full[0:1, NC:NC + 1] / count, (8, LANES))
     arrived(qy.at[pl.ds(0, Y - 1)], rsem.at[E_QY])
-    for d in (1, 3, 2):
-        send(qy, qx.at[x], ssem.at[E_QX], rsem.at[E_QX], at_x((x + d) % X))
-    qx[x] = qy[...]
+    for d in (2, 1, 3):
+        send(qy, qxy.at[x], ssem.at[E_QXY], rsem.at[E_QXY], at_x((x + d) % X))
+    qxy[x] = qy[...]
     arrived(qx.at[pl.ds(0, X - 1)], rsem.at[E_QX])
+    for d in (2, 1, 3):
+        send(qx, qyx.at[y], ssem.at[E_QYX], rsem.at[E_QYX], at_y((y + d) % Y))
+    qyx[y] = qx[...]
+    arrived(qxy.at[pl.ds(0, X - 1)], rsem.at[E_QXY])
+    arrived(qyx.at[pl.ds(0, Y - 1)], rsem.at[E_QYX])
     for yb in range(Y):
-        part = qx[:, yb].reshape(HB // 2, LANES).T
+        part = jnp.concatenate([qxy[:, yb], qyx[yb]], axis=1).reshape(HB // 2, LANES).T
         dw1_out[:, yb * HB:yb * HB + HB // 2] = part[0:F]
         dw1_out[:, yb * HB + HB // 2:(yb + 1) * HB] = part[LANES // 2:LANES // 2 + F]
 
@@ -521,6 +546,8 @@
     sent(qz.at[pl.ds(0, Z - 1)], ssem.at[E_QZ])
     sent(qy.at[pl.ds(0, Y - 1)], ssem.at[E_QY])
     sent(qx.at[pl.ds(0, X - 1)], ssem.at[E_QX])
+    sent(qxy.at[pl.ds(0, X - 1)], ssem.at[E_QXY])
+    sent(qyx.at[pl.ds(0, Y - 1)], ssem.at[E_QYX])
 
 
 def solution(mesh):
@@ -538,7 +565,7 @@
         HB = H // Y
         HU = HB // NV
         NCH = Y * S
-        assert R == Z * Y and CB == S * I and F + 2 <= LANES // 2 and NC < LANES
+        assert R == Z * Y and CB == S * I and X == Y and F + 2 <= LANES // 2 and NC < LANES
         vm = pltpu.VMEM
         dma = pltpu.SemaphoreType.DMA
         scratch = [
@@ -576,9 +603,9 @@
             vm((Y, S, HB), BF),
             vm((Y, S, HB), BF),
             vm((NV, Z, Y, S, HU), BF),
-            vm((NV, HU, Z * Y * S), BF),
-            vm((NV, X, C, HU, NCH), F32),
-            vm((NV, X, HU, NCH), F32),
+            vm((NV // 2, 2 * HU, Z * Y * S), BF),
+            vm((NV // 2, X, C, 2 * HU, NCH), F32),
+            vm((NV // 2, X, 2 * HU, NCH), F32),
             vm((NV, 2, HU // 2, NCH), F32),
             vm((NV, 2, HU, NCH), F32),
             vm((C, X, Y, Z, 8, LANES), F32),
@@ -597,8 +624,10 @@
             vm((Z, 8, LANES), F32),
             vm((8, LANES), F32),
             vm((Z, 8, LANES), F32),
-            vm((Y, Z, 8, LANES), F32),
-            vm((X, Y, Z, 8, LANES), F32),
+            vm((Y, Z // 2, 8, LANES), F32),
+            vm((X, Z // 2, 8, LANES), F32),
+            vm((X, Y, Z // 2, 8, LANES), F32),
+            vm((Y, X, Z // 2, 8, LANES), F32),
             dma((NSEM,)),
             dma((NSEM,)),
             dma((Y - 1, Z)),
@@ -617,7 +646,7 @@
             in_specs=[aspec, vspec, vspec, vspec, aspec, aspec],
             out_specs=(vspec, vspec, vspec),
             scratch_shapes=scratch,
-            compiler_params=pltpu.CompilerParams(collective_id=0, has_side_effects=True, vmem_limit_bytes=62 * 1024 * 1024),
+            compiler_params=pltpu.CompilerParams(collective_id=0, has_side_effects=True, vmem_limit_bytes=52 * 1024 * 1024),
             name="gcn_step",
         )(adj_blk.reshape(Z, Y, S, CB), feat_blk.T, label_blk[None, :], mask_blk[None, :], w_one, w_two)
         return loss[0, 0], dw_one, dw_two

time: 183 us -> 179 us (0.978)
  Pallas kernels: 177 us -> 172 us
    pallas_call x1, Pallas kernels: 177 us -> 172 us  [device_step(): pl.pallas_call(functools.partial(_step, (Z, Y, X, C, S, CB, H, F, NC)), o...]
    unnamed x2 -> x10, local copies, waits for them, and re-layouts: 4.08 us -> 4.77 us
where the time goes in v4:
time: 179 us; the launch traced here: 178 us
  Pallas kernels  172 us (96%)
  local copies, waits for them, and re-layouts  5.28 us (3%)
    pallas_call x1, Pallas kernels, device_step(): pl.pallas_call(functools.partial(_step, (Z, Y, X, C, S, CB, H, F, NC)), o...  172 us
    unnamed x10, local copies, waits for them, and re-layouts  4.77 us

profile of v4, /device:TPU:2, one launch (start us, length us, event | category | flops | bytes accessed | tf_op | source)
XLA Modules:
  0.0 177.6 jit_solution(13834333429609795734)
XLA Ops:
  0.6 0.0 copy-start
  0.6 1.0 copy-done
  1.7 0.0 copy-start.1
  1.7 0.7 copy-done.1
  2.4 0.0 copy-start.2
  2.4 0.7 copy-done.2
  3.0 0.0 copy-start.3
  3.0 0.7 copy-done.3
  3.7 171.7 %gcn_step.1 = (f32[50,2048]{1,0:T(8,128)S(1)}, f32[2048,121]{1,0:T(8,128)S(1)}, f32[8,128]{1,0:T(8,128)S(1)}) custom-call(bf16[8,4,64,512]{3,2,1,0:T(8,128)(2,1)} %bitcast.8, bf16[50,64]{1,0:T(8,128)(2,1)S(1)} %bitcast.5, s32[1,64]{1,0:T(1,128)S(1)} %bitcast.6, s32[1,64]{1,0:T(1,128)S(1)} %bitcast.7, f32[50,2048]{1,0:T(8,128)S(1)} %copy-done, f32[2048,121]{1,0:T(8,128)} %w_two.1), custom_call_target="tpu_custom_call" | custom-call | tf_op jit(solution)/shard_map/gcn_step/pallas_call | solution.py:643
  175.4 0.5 slice.3
  175.9 0.8 copy.11
  176.6 1.0 copy.12
Async XLA Ops:
  0.6 1.0 copy-start
  1.7 0.7 copy-start.1
  2.4 0.7 copy-start.2
  3.0 0.7 copy-start.3

commit v5 on v4

--- a/solution.py
+++ b/solution.py
@@ -13,13 +13,13 @@
 LANES = 128
 NSUB = 4
 NV = 4
-NSEM = 41
+NSEM = 44
 BF = jnp.bfloat16
 F32 = jnp.float32
 
 
-def _step(dims, a_hbm, feat, lab, msk, w_one, w_two, dw1_out, dw2_out, loss_out,
-          af, mt, mtt, w1f, w2f, w1, w2, w2t, xs, xp, y1, cs, cr, sb, rb, z1, h1, y2, yp, zp, zr, g2, gr, dp, rc, rx, ry, ry2, rx2d,
+def _step(dims, a_hbm, feat_hbm, lab_hbm, msk_hbm, w_one, w_two, dw1_out, dw2_out, loss_out,
+          af, feat, lab, msk, mt, mtt, w1f, w2f, w1, w2, w2t, xs, xp, y1, cs, cr, sb, rb, z1, h1, y2, yp, zp, zr, g2, gr, dp, rc, rx, ry, ry2, rx2d,
           d2, dg, ms, mk, gz, gt, dy, rcy, rx1, rx2, wb, wc, wx, wy, wz, wf, oz, oy, ox, oc, pb, pc, px, pz, pf, qz, qy, qx, qxy, qyx,
           ssem, rsem, rsem_a, rsem_b, rsem_f, rsem_ring, rsem_ag, rsem_c, rsem_x):
     Z, Y, X, C, S, CB, H, F, NC = dims
@@ -79,11 +79,15 @@
 
     (E_X, E_XC, E_A, E_B, E_F, E_RING, E_CNT, E_Y2, E_Y2C, E_Z2, E_G2, E_DC, E_DX, E_DY, E_AG, E_RC, E_RX, E_RX2,
      E_WC, E_WX, E_WY, E_WZ, E_OZ, E_OY, E_OX, E_OC, E_PC, E_PX, E_PZ, E_QZ, E_QY, E_QX, E_LA, E_L1, E_L2,
-     E_M, E_DY2, E_DX2, E_DG, E_QXY, E_QYX) = range(NSEM)
+     E_M, E_DY2, E_DX2, E_DG, E_QXY, E_QYX, E_IN, E_IN1, E_IN2) = range(NSEM)
 
     load_a = pltpu.make_async_copy(a_hbm, af.at[y], ssem.at[E_LA])
     load_1 = pltpu.make_async_copy(w_one, w1f, ssem.at[E_L1])
     load_2 = pltpu.make_async_copy(w_two, w2f, ssem.at[E_L2])
+    loads = [pltpu.make_async_copy(src, dst, ssem.at[E_IN + k]) for k, (src, dst) in
+             enumerate(((feat_hbm, feat), (lab_hbm, lab), (msk_hbm, msk)))]
+    for load in loads:
+        load.start()
     load_a.start()
     load_1.start()
     load_2.start()
@@ -99,6 +103,8 @@
     lax.fori_loop(1, NQ, greet_plane, 0)
     pl.semaphore_signal(bar, inc=1, device_id=partner, device_id_type=pl.DeviceIdType.MESH)
 
+    for load in loads:
+        load.wait()
     mt[...] = jnp.zeros_like(mt)
     mt[0:F] = feat[...].astype(F32)
     mt[F:F + 1] = msk[...].astype(F32)
@@ -165,44 +171,51 @@
         for d in range(1, Y):
             arrived(af.at[0, 0, 0], rsem_a.at[d - 1, zc])
 
-    def ring(t, u):
-        s, j = t // (2 * NSUB), t % (2 * NSUB)
+    def columns(j):
+        return pl.ds(pl.multiple_of(j * HR, HR), HR)
+
+    def products(s, j):
         up = j % 2 == 0
         dest = lax.rem(jnp.where(up, z - 1 - s, z + 1 + s) + 2 * Z, Z)
-        nb = lax.rem(jnp.where(up, z + 1, z - 1) + Z, Z)
-        col = pl.multiple_of(j * HR, HR)
         fresh = ((j == 0) & ((s < half) | (s == Z - 1))) | ((j == 1) & (s < half - 1))
-
-        @pl.when(s == 0)
-        def _():
-            for yb in range(Y):
-                rows = plane_rows(xp, yb)
-                y1[yb * CB:(yb + 1) * CB, pl.ds(col, HR)] = dot(rows, w1[:, pl.ds(col, HR)]).astype(BF)
 
         @pl.when(fresh)
         def _():
             wait_a(dest)
 
-        acc = dot(af[0, dest, y], y1[pl.ds(0, CB), pl.ds(col, HR)])
+        acc = dot(af[0, dest, y], y1[pl.ds(0, CB), columns(j)])
         for yb in range(1, Y):
-            acc = acc + dot(af[yb, dest, y], y1[pl.ds(yb * CB, CB), pl.ds(col, HR)])
-        z1[:, pl.ds(col, HR)] = acc
-
-        @pl.when(s > 0)
-        def _():
-            prev = jnp.maximum(s - 1, 0)
-            arrived(rb.at[0, 0], rsem_ring.at[j, prev])
-            z1[:, pl.ds(col, HR)] = z1[:, pl.ds(col, HR)] + rb[j, prev]
-
-        @pl.when(s < Z - 1)
-        def _():
-            here = jnp.minimum(s, Z - 2)
-            sb[j, here] = z1[:, pl.ds(col, HR)]
-            send(sb.at[j, here], rb.at[j, here], ssem.at[E_RING], rsem_ring.at[j, here], at_z(nb))
-
+            acc = acc + dot(af[yb, dest, y], y1[pl.ds(yb * CB, CB), columns(j)])
+        return acc
+
+    def pass_on(s, j):
+        nb = lax.rem(jnp.where(j % 2 == 0, z + 1, z - 1) + Z, Z)
+        send(sb.at[j, s], rb.at[j, s], ssem.at[E_RING], rsem_ring.at[j, s], at_z(nb))
+
+    def ring_first(j, u):
+        for yb in range(Y):
+            y1[yb * CB:(yb + 1) * CB, columns(j)] = dot(plane_rows(xp, yb), w1[:, columns(j)]).astype(BF)
+        sb[j, 0] = products(0, j)
+        pass_on(0, j)
         return u
 
-    lax.fori_loop(0, Z * 2 * NSUB, ring, 0)
+    def ring_next(t, u):
+        s, j = t // (2 * NSUB) + 1, t % (2 * NSUB)
+        acc = products(s, j)
+        arrived(rb.at[0, 0], rsem_ring.at[j, s - 1])
+        sb[j, s] = acc + rb[j, s - 1]
+        pass_on(s, j)
+        return u
+
+    def ring_last(j, u):
+        acc = products(Z - 1, j)
+        arrived(rb.at[0, 0], rsem_ring.at[j, Z - 2])
+        z1[:, columns(j)] = acc + rb[j, Z - 2]
+        return u
+
+    lax.fori_loop(0, 2 * NSUB, ring_first, 0)
+    lax.fori_loop(0, (Z - 2) * 2 * NSUB, ring_next, 0)
+    lax.fori_loop(0, 2 * NSUB, ring_last, 0)
 
     h1[...] = jnp.maximum(z1[...], 0.0).astype(BF)
     y2[...] = dot(h1[...], w2[...]).astype(BF)
@@ -314,32 +327,33 @@
     def piece(v):
         return pl.ds(v % 2 * HU, HU)
 
-    def product(p):
+    def prepare(p):
         for v in (2 * p, 2 * p + 1):
             for d in range(2):
                 arrived(gz.at[v, 0, pl.ds(0, Y // 2)], rsem_ag.at[v, d, half])
             for k in range(Z):
                 gt[p, piece(v), k * Y * S:(k + 1) * Y * S] = gz[v, k].reshape(Y * S, HU).T
 
-        def chunk(core):
-            def body(k, u):
-                yb = lax.rem(y + k + jnp.where(k == 2, 1, 0) - jnp.where(k == 3, 1, 0), Y)
-                q = yb * C + core
-                off = pl.multiple_of(core * NCH, NCH)
-                dy[p, q // C, core] = dot(gt[p], af[yb, :, :, :, pl.ds(off, NCH)].reshape(Z * Y * S, NCH))
-                return u
-            return body
-
-        first = Y - 1 if p == 0 else 0
-        lax.fori_loop(0, first, chunk(1 - c), 0)
-        if p == 0:
+    def chunks(p, lo, hi):
+        def chunk(n, u):
+            k = n % Y
+            core = jnp.where(n < Y, 1 - c, c)
+            yb = lax.rem(y + k + jnp.where(k == 2, 1, 0) - jnp.where(k == 3, 1, 0), Y)
+            off = pl.multiple_of(core * NCH, NCH)
+            dy[p, yb, core] = dot(gt[p], af[yb, :, :, :, pl.ds(off, NCH)].reshape(Z * Y * S, NCH))
+            return u
+
+        if p == 0 and lo < Y <= hi:
+            lax.fori_loop(lo, Y - 1, chunk, 0)
             for d in (1, 3):
                 for k in range(1, Y):
                     arrived(af.at[0, pl.ds(0, half), 0], rsem_f.at[d // 2, k - 1])
-        lax.fori_loop(first, Y, chunk(1 - c), 0)
+            lo = Y - 1
+        lax.fori_loop(lo, hi, chunk, 0)
+
+    def send_core(p):
         for v in (2 * p, 2 * p + 1):
             send(dy.at[p, :, 1 - c, piece(v)], rcy.at[p, :, piece(v)], ssem.at[E_RC], rsem_c.at[v], partner)
-        lax.fori_loop(0, Y, chunk(c), 0)
 
     nxt, prv, opp = (x + 1) % X, (x + X - 1) % X, (x + 2) % X
     hh = HU // 2
@@ -451,14 +465,14 @@
         (gather_step, 0, 2), (gather_step, 1, 2), (w_core,)]
     for t in range(3, half + 1):
         steps += [(gather_step, 0, t), (gather_step, 1, t)]
-    steps += [(gather_step, 2, 1), (gather_step, 3, 1), (product, 0), (gather_step, 2, 2), (gather_step, 3, 2), (w_x,), (reduce_core, 0),
-              (reduce_core, 1)]
+    steps += [(gather_step, 2, 1), (gather_step, 3, 1), (prepare, 0), (chunks, 0, 0, 2), (gather_step, 2, 2), (gather_step, 3, 2),
+              (chunks, 0, 2, 4), (send_core, 0), (chunks, 0, 4, 6)]
     for t in range(3, half + 1):
         steps += [(gather_step, 2, t), (gather_step, 3, t)]
         if t == 3:
-            steps += [(reduce_x, 0), (w_y,), (reduce_x, 1)]
-    steps += [(product, 1), (reduce_core, 2), (reduce_core, 3), (grad_one, 0), (grad_one, 1), (reduce_x, 2), (reduce_x, 3), (w_z,),
-              (o_z,), (grad_one, 2), (grad_one, 3)]
+            steps += [(chunks, 0, 6, 8), (w_x,), (reduce_core, 0), (reduce_core, 1)]
+    steps += [(reduce_x, 0), (reduce_x, 1), (w_y,), (prepare, 1), (chunks, 1, 0, 4), (send_core, 1), (chunks, 1, 4, 8), (reduce_core, 2),
+              (reduce_core, 3), (grad_one, 0), (grad_one, 1), (w_z,), (reduce_x, 2), (reduce_x, 3), (o_z,), (grad_one, 2), (grad_one, 3)]
     for step in steps:
         step[0](*step[1:])
 
@@ -570,6 +584,9 @@
         dma = pltpu.SemaphoreType.DMA
         scratch = [
             vm((Y, Z, Y, S, CB), BF),
+            vm((F, S), BF),
+            vm((1, S), jnp.int32),
+            vm((1, S), jnp.int32),
             vm((LANES, S), F32),
             vm((S, LANES), F32),
             vm((F, H), F32),
@@ -639,11 +656,11 @@
             dma((NV, 4)),
         ]
         vspec = pl.BlockSpec(memory_space=pltpu.VMEM)
-        aspec = pl.BlockSpec(memory_space=pl.ANY)
+        aspec = pl.BlockSpec(memory_space=pltpu.HBM)
         dw_one, dw_two, loss = pl.pallas_call(
             functools.partial(_step, (Z, Y, X, C, S, CB, H, F, NC)),
             out_shape=(jax.ShapeDtypeStruct((F, H), F32), jax.ShapeDtypeStruct((H, NC), F32), jax.ShapeDtypeStruct((8, LANES), F32)),
-            in_specs=[aspec, vspec, vspec, vspec, aspec, aspec],
+            in_specs=[aspec] * 6,
             out_specs=(vspec, vspec, vspec),
             scratch_shapes=scratch,
             compiler_params=pltpu.CompilerParams(collective_id=0, has_side_effects=True, vmem_limit_bytes=52 * 1024 * 1024),

time: 179 us -> 177 us (0.989)
  Pallas kernels: 172 us -> 170 us
where the time goes in v5:
time: 177 us; the launch traced here: 176 us
  Pallas kernels  170 us (96%)
  local copies, waits for them, and re-layouts  5.28 us (3%)
    pallas_call x1, Pallas kernels, device_step(): pl.pallas_call(functools.partial(_step, (Z, Y, X, C, S, CB, H, F, NC)), o...  170 us
    unnamed x10, local copies, waits for them, and re-layouts  4.77 us

profile of v5, /device:TPU:2, one launch (start us, length us, event | category | flops | bytes accessed | tf_op | source)
XLA Modules:
  0.0 176.2 jit_solution(4259115798666499857)
XLA Ops:
  0.6 0.0 copy-start
  0.6 1.0 copy-done
  1.7 0.0 copy-start.1
  1.7 0.7 copy-done.1
  2.4 0.0 copy-start.2
  2.4 0.7 copy-done.2
  3.0 0.0 copy-start.3
  3.0 0.7 copy-done.3
  3.7 170.3 %gcn_step.1 = (f32[50,2048]{1,0:T(8,128)S(1)}, f32[2048,121]{1,0:T(8,128)S(1)}, f32[8,128]{1,0:T(8,128)S(1)}) custom-call(bf16[8,4,64,512]{3,2,1,0:T(8,128)(2,1)} %bitcast.8, bf16[50,64]{1,0:T(8,128)(2,1)S(1)} %bitcast.5, s32[1,64]{1,0:T(1,128)S(1)} %bitcast.6, s32[1,64]{1,0:T(1,128)S(1)} %bitcast.7, f32[50,2048]{1,0:T(8,128)S(1)} %copy-done, f32[2048,121]{1,0:T(8,128)} %w_two.1), custom_call_target="tpu_custom_call" | custom-call | tf_op jit(solution)/shard_map/gcn_step/pallas_call | solution.py:660
  174.0 0.5 slice.3
  174.5 0.8 copy.11
  175.2 1.0 copy.12
Async XLA Ops:
  0.6 1.0 copy-start
  1.7 0.7 copy-start.1
  2.4 0.7 copy-start.2
  3.0 0.7 copy-start.3

commit v6 on v5

--- a/solution.py
+++ b/solution.py
@@ -13,14 +13,14 @@
 LANES = 128
 NSUB = 4
 NV = 4
-NSEM = 44
+NSEM = 46
 BF = jnp.bfloat16
 F32 = jnp.float32
 
 
 def _step(dims, a_hbm, feat_hbm, lab_hbm, msk_hbm, w_one, w_two, dw1_out, dw2_out, loss_out,
           af, feat, lab, msk, mt, mtt, w1f, w2f, w1, w2, w2t, xs, xp, y1, cs, cr, sb, rb, z1, h1, y2, yp, zp, zr, g2, gr, dp, rc, rx, ry, ry2, rx2d,
-          d2, dg, ms, mk, gz, gt, dy, rcy, rx1, rx2, wb, wc, wx, wy, wz, wf, oz, oy, ox, oc, pb, pc, px, pz, pf, qz, qy, qx, qxy, qyx,
+          d2, dg, ms, mk, gz, gt, dy, rcy, rx1, rx2, wb, wc, wx, wy, wz, wf, oz, oy, ox, oc, pb, px, pz, pf, qz, qy, qx, qxy, qyx,
           ssem, rsem, rsem_a, rsem_b, rsem_f, rsem_ring, rsem_ag, rsem_c, rsem_x):
     Z, Y, X, C, S, CB, H, F, NC = dims
     I = X * C
@@ -77,8 +77,8 @@
             acc = acc + ref[k]
         return acc
 
-    (E_X, E_XC, E_A, E_B, E_F, E_RING, E_CNT, E_Y2, E_Y2C, E_Z2, E_G2, E_DC, E_DX, E_DY, E_AG, E_RC, E_RX, E_RX2,
-     E_WC, E_WX, E_WY, E_WZ, E_OZ, E_OY, E_OX, E_OC, E_PC, E_PX, E_PZ, E_QZ, E_QY, E_QX, E_LA, E_L1, E_L2,
+    (E_X, E_XC, E_A, E_B, E_F, E_RING, E_CNT, E_Y2, E_Y2C, E_Z2, E_G2, E_DC, E_DC1, E_DC2, E_DC3, E_DX, E_DY, E_AG, E_RC, E_RX, E_RX2,
+     E_WC, E_WX, E_WY, E_WZ, E_OZ, E_OY, E_OX, E_OC, E_PX, E_PZ, E_QZ, E_QY, E_QX, E_LA, E_L1, E_L2,
      E_M, E_DY2, E_DX2, E_DG, E_QXY, E_QYX, E_IN, E_IN1, E_IN2) = range(NSEM)
 
     load_a = pltpu.make_async_copy(a_hbm, af.at[y], ssem.at[E_LA])
@@ -165,14 +165,26 @@
 
     arrived(most(xp), rsem.at[E_X])
     send(xp.at[c], xp.at[c], ssem.at[E_XC], rsem.at[E_XC], partner)
+
+    def columns(j):
+        return pl.ds(pl.multiple_of(j * HR, HR), HR)
+
+    def y1_half(k, j):
+        y1[:, k, :, columns(j)] = dot(xp[k].reshape(NQ * S, LANES), w1[:, columns(j)]).astype(BF).reshape(NQ, S, HR)
+
+    def y1_own(j, u):
+        y1_half(c, j)
+        return u
+
+    def y1_block(yb, j):
+        return y1[yb * X:(yb + 1) * X, :, :, columns(j)].reshape(CB, HR)
+
+    lax.fori_loop(0, 2 * NSUB, y1_own, 0)
     arrived(xp.at[0], rsem.at[E_XC])
 
     def wait_a(zc):
         for d in range(1, Y):
             arrived(af.at[0, 0, 0], rsem_a.at[d - 1, zc])
-
-    def columns(j):
-        return pl.ds(pl.multiple_of(j * HR, HR), HR)
 
     def products(s, j):
         up = j % 2 == 0
@@ -183,9 +195,9 @@
         def _():
             wait_a(dest)
 
-        acc = dot(af[0, dest, y], y1[pl.ds(0, CB), columns(j)])
+        acc = dot(af[0, dest, y], y1_block(0, j))
         for yb in range(1, Y):
-            acc = acc + dot(af[yb, dest, y], y1[pl.ds(yb * CB, CB), columns(j)])
+            acc = acc + dot(af[yb, dest, y], y1_block(yb, j))
         return acc
 
     def pass_on(s, j):
@@ -193,8 +205,7 @@
         send(sb.at[j, s], rb.at[j, s], ssem.at[E_RING], rsem_ring.at[j, s], at_z(nb))
 
     def ring_first(j, u):
-        for yb in range(Y):
-            y1[yb * CB:(yb + 1) * CB, columns(j)] = dot(plane_rows(xp, yb), w1[:, columns(j)]).astype(BF)
+        y1_half(1 - c, j)
         sb[j, 0] = products(0, j)
         pass_on(0, j)
         return u
@@ -237,15 +248,19 @@
     arrived(most(yp), rsem.at[E_Y2])
     send(yp.at[c], yp.at[c], ssem.at[E_Y2C], rsem.at[E_Y2C], partner)
     arrived(yp.at[0], rsem.at[E_Y2C])
+    def z2_part(zq):
+        part = dot(af[0, zq, y], plane_rows(yp, 0))
+        for yb in range(1, Y):
+            part = part + dot(af[yb, zq, y], plane_rows(yp, yb))
+        return part
+
+    for d in far:
+        zq = (z + d) % Z
+        zp[zq] = z2_part(zq)
+        send(zp.at[zq], zr.at[z], ssem.at[E_Z2], rsem.at[E_Z2], at_z(zq))
+    zr[z] = z2_part(z)
     for yb in range(Y):
         ms[yb] = jnp.where(z1[:, yb * HB:(yb + 1) * HB] > 0.0, 1.0, 0.0).astype(BF)
-    for yb in range(Y):
-        part = dot(af[yb, :, y].reshape(Z * S, CB), plane_rows(yp, yb)).reshape(Z, S, LANES)
-        zp[...] = part if yb == 0 else zp[...] + part
-    for d in far:
-        zq = (z + d) % Z
-        send(zp.at[zq], zr.at[z], ssem.at[E_Z2], rsem.at[E_Z2], at_z(zq))
-    zr[z] = zp[z]
     for d in (2, 1, 3):
         yq = (y + d) % Y
         send(ms.at[yq], mk.at[y], ssem.at[E_M], rsem.at[E_M], at_y(yq))
@@ -277,9 +292,10 @@
     for yb in range(Y):
         part = dot(g2t, af[yb, :, y].reshape(Z * S, CB))
         dp[yb] = part.T.reshape(X, C, S, LANES)
-    send(dp.at[:, :, 1 - c], rc, ssem.at[E_DC], rsem.at[E_DC], partner)
-    arrived(rc, rsem.at[E_DC])
-    rc[...] = rc[...] + dp[:, :, c]
+        send(dp.at[yb, :, 1 - c], rc.at[yb], ssem.at[E_DC + yb], rsem.at[E_DC + yb], partner)
+    for yb in range(Y):
+        arrived(rc.at[yb], rsem.at[E_DC + yb])
+        rc[yb] = rc[yb] + dp[yb, :, c]
     sh = S // 2
     for d in (2, 1, 3):
         xq, yq = (x + d) % X, (y + d) % Y
@@ -470,28 +486,27 @@
     for t in range(3, half + 1):
         steps += [(gather_step, 2, t), (gather_step, 3, t)]
         if t == 3:
-            steps += [(chunks, 0, 6, 8), (w_x,), (reduce_core, 0), (reduce_core, 1)]
-    steps += [(reduce_x, 0), (reduce_x, 1), (w_y,), (prepare, 1), (chunks, 1, 0, 4), (send_core, 1), (chunks, 1, 4, 8), (reduce_core, 2),
+            steps += [(chunks, 0, 6, 8), (w_x,)]
+    steps += [(reduce_core, 0), (reduce_core, 1), (reduce_x, 0), (reduce_x, 1), (w_y,), (prepare, 1), (chunks, 1, 0, 4), (send_core, 1), (chunks, 1, 4, 8), (reduce_core, 2),
               (reduce_core, 3), (grad_one, 0), (grad_one, 1), (w_z,), (reduce_x, 2), (reduce_x, 3), (o_z,), (grad_one, 2), (grad_one, 3)]
     for step in steps:
         step[0](*step[1:])
 
-    send(pb, pc, ssem.at[E_PC], rsem.at[E_PC], partner)
-    arrived(pc, rsem.at[E_PC])
-    pc[...] = pc[...] + pb[...]
     for d in (2, 1, 3):
         xq = (x + d) % X
-        send(pc.at[xq], px.at[x], ssem.at[E_PX], rsem.at[E_PX], at_x(xq))
-    px[x] = pc[x]
+        send(pb.at[xq], px.at[x], ssem.at[E_PX], rsem.at[E_PX], at_x(xq))
+    px[x] = pb[x]
     o_y()
     arrived(px.at[pl.ds(0, X - 1)], rsem.at[E_PX])
     px[x] = added(px, X)
     for d in far:
         zq = (z + d) % Z
-        send(px.at[x, zq], pz.at[z], ssem.at[E_PZ], rsem.at[E_PZ], at_z(zq))
-    pz[z] = px[x, z]
-    arrived(pz.at[pl.ds(0, Z - 1)], rsem.at[E_PZ])
-    pf[...] = added(pz, Z)
+        for k in range(C):
+            send(px.at[x, zq], pz.at[c * Z + z], ssem.at[E_PZ], rsem.at[E_PZ], (zq * Y + y, x * C + k))
+    send(px.at[x, z], pz.at[c * Z + z], ssem.at[E_PZ], rsem.at[E_PZ], partner)
+    pz[c * Z + z] = px[x, z]
+    arrived(pz.at[pl.ds(0, C * Z - 1)], rsem.at[E_PZ])
+    pf[...] = added(pz, C * Z)
     for d in far:
         send(pf, qz.at[z], ssem.at[E_QZ], rsem.at[E_QZ], at_z((z + d) % Z))
     qz[z] = pf[...]
@@ -535,7 +550,8 @@
     sent(yp.at[0], ssem.at[E_Y2C])
     sent(zr.at[pl.ds(0, Z - 1)], ssem.at[E_Z2])
     sent(gr.at[pl.ds(0, Z - 1)], ssem.at[E_G2])
-    sent(rc, ssem.at[E_DC])
+    for yb in range(Y):
+        sent(rc.at[yb], ssem.at[E_DC + yb])
     sent(rx.at[pl.ds(0, X - 1)], ssem.at[E_DX])
     sent(ry.at[pl.ds(0, Y - 1)], ssem.at[E_DY])
     sent(ry2.at[pl.ds(0, Y - 1)], ssem.at[E_DY2])
@@ -554,9 +570,8 @@
     sent(oy.at[pl.ds(0, Y - 1)], ssem.at[E_OY])
     sent(ox.at[pl.ds(0, X - 1)], ssem.at[E_OX])
     sent(oc.at[0], ssem.at[E_OC])
-    sent(pc, ssem.at[E_PC])
     sent(px.at[pl.ds(0, X - 1)], ssem.at[E_PX])
-    sent(pz.at[pl.ds(0, Z - 1)], ssem.at[E_PZ])
+    sent(pz.at[pl.ds(0, C * Z - 1)], ssem.at[E_PZ])
     sent(qz.at[pl.ds(0, Z - 1)], ssem.at[E_QZ])
     sent(qy.at[pl.ds(0, Y - 1)], ssem.at[E_QY])
     sent(qx.at[pl.ds(0, X - 1)], ssem.at[E_QX])
@@ -596,7 +611,7 @@
             vm((LANES, H), BF),
             vm((S, LANES), BF),
             vm((C, NQ, S, LANES), BF),
-            vm((Y * CB, H), BF),
+            vm((NQ, C, S, H), BF),
             vm((8, LANES), F32),
             vm((Z, 8, LANES), F32),
             vm((2 * NSUB, Z - 1, S, HR), F32),
@@ -637,8 +652,7 @@
             vm((C, X, Y, Z, 8, LANES), F32),
             vm((X, Z, 8, LANES), F32),
             vm((X, Z, 8, LANES), F32),
-            vm((X, Z, 8, LANES), F32),
-            vm((Z, 8, LANES), F32),
+            vm((C * Z, 8, LANES), F32),
             vm((8, LANES), F32),
             vm((Z, 8, LANES), F32),
             vm((Y, Z // 2, 8, LANES), F32),
@@ -657,6 +671,7 @@
         ]
         vspec = pl.BlockSpec(memory_space=pltpu.VMEM)
         aspec = pl.BlockSpec(memory_space=pltpu.HBM)
+        operands = (adj_blk.reshape(Z, Y, S, CB), feat_blk.T, label_blk[None, :], mask_blk[None, :], w_one, w_two)
         dw_one, dw_two, loss = pl.pallas_call(
             functools.partial(_step, (Z, Y, X, C, S, CB, H, F, NC)),
             out_shape=(jax.ShapeDtypeStruct((F, H), F32), jax.ShapeDtypeStruct((H, NC), F32), jax.ShapeDtypeStruct((8, LANES), F32)),
@@ -665,7 +680,7 @@
             scratch_shapes=scratch,
             compiler_params=pltpu.CompilerParams(collective_id=0, has_side_effects=True, vmem_limit_bytes=52 * 1024 * 1024),
             name="gcn_step",
-        )(adj_blk.reshape(Z, Y, S, CB), feat_blk.T, label_blk[None, :], mask_blk[None, :], w_one, w_two)
+        )(*[pltpu.with_memory_space_constraint(v, pltpu.HBM) for v in operands])
         return loss[0, 0], dw_one, dw_two
 
     return jax.shard_map(device_step, mesh=mesh, in_specs=(P(None, "nodes", "rep"), row_spec, P(), P(), row_spec, row_spec), out_specs=(P(), P(), P()), check_vma=False)

time: 177 us -> 173 us (0.977)
  local copies, waits for them, and re-layouts: 5.28 us -> 2.25 us
    unnamed x10 -> x2, local copies, waits for them, and re-layouts: 4.77 us -> 1.74 us
where the time goes in v6:
time: 173 us; the launch traced here: 172 us
  Pallas kernels  169 us (98%)
  local copies, waits for them, and re-layouts  2.25 us (1%)
    pallas_call x1, Pallas kernels, device_step(): pl.pallas_call(functools.partial(_step, (Z, Y, X, C, S, CB, H, F, NC)), o...  169 us

profile of v6, /device:TPU:2, one launch (start us, length us, event | category | flops | bytes accessed | tf_op | source)
XLA Modules:
  0.0 172.4 jit_solution(14923106460177202450)
XLA Ops:
  0.6 169.5 %gcn_step.1 = (f32[50,2048]{1,0:T(8,128)S(1)}, f32[2048,121]{1,0:T(8,128)S(1)}, f32[8,128]{1,0:T(8,128)S(1)}) custom-call(bf16[8,4,64,512]{3,2,1,0:T(8,128)(2,1)} %bitcast.5, bf16[50,64]{1,0:T(8,128)(2,1)} %bitcast.6, s32[1,64]{1,0:T(1,128)} %bitcast.7, s32[1,64]{1,0:T(1,128)} %bitcast.8, f32[50,2048]{1,0:T(8,128)} %w_one.1, f32[2048,121]{1,0:T(8,128)} %w_two.1), custom_call_target="tpu_custom_call" | custom-call | tf_op jit(solution)/shard_map/gcn_step/pallas_call | solution.py:675
  170.1 0.5 slice.3
  170.6 0.8 copy.11
  171.4 1.0 copy.12

commit v7 on v6

--- a/solution.py
+++ b/solution.py
@@ -19,7 +19,7 @@
 
 
 def _step(dims, a_hbm, feat_hbm, lab_hbm, msk_hbm, w_one, w_two, dw1_out, dw2_out, loss_out,
-          af, feat, lab, msk, mt, mtt, w1f, w2f, w1, w2, w2t, xs, xp, y1, cs, cr, sb, rb, z1, h1, y2, yp, zp, zr, g2, gr, dp, rc, rx, ry, ry2, rx2d,
+          af, feat, lab, msk, mt, mtt, w1f, w2f, w1, w2, w2t, xs, xp, xn, y1, cs, cr, sb, rb, z1, h1, y2, yp, zp, zr, g2, gr, dp, rc, rx, ry, ry2, rx2d,
           d2, dg, ms, mk, gz, gt, dy, rcy, rx1, rx2, wb, wc, wx, wy, wz, wf, oz, oy, ox, oc, pb, px, pz, pf, qz, qy, qx, qxy, qyx,
           ssem, rsem, rsem_a, rsem_b, rsem_f, rsem_ring, rsem_ag, rsem_c, rsem_x):
     Z, Y, X, C, S, CB, H, F, NC = dims
@@ -71,6 +71,9 @@
     def plane_rows(ref, yb):
         return jnp.stack([ref[k, yb * X:(yb + 1) * X] for k in range(C)], axis=1).reshape(CB, LANES)
 
+    def turned(v):
+        return jnp.concatenate([v[:, LANES // 2:], v[:, 0:LANES // 2]], axis=1)
+
     def added(ref, n):
         acc = ref[0]
         for k in range(1, n):
@@ -110,7 +113,7 @@
     mt[F:F + 1] = msk[...].astype(F32)
     mt[F + 1:F + 2] = lab[...].astype(F32)
     mtt[...] = mt[...].T
-    xs[...] = mtt[...].astype(BF)
+    xs[...] = (mtt[0:S // 2] + turned(mtt[S // 2:S])).astype(BF)
     pl.semaphore_wait(bar, NQ + Z - 1)
 
     def send_x(d, u):
@@ -155,7 +158,8 @@
 
     load_1.wait()
     w1[...] = jnp.zeros_like(w1)
-    w1[0:F] = w1f[...].astype(BF)
+    w1[0, 0:F] = w1f[...].astype(BF)
+    w1[1, LANES // 2:LANES // 2 + F] = w1f[...].astype(BF)
     load_2.wait()
     w2[...] = jnp.zeros_like(w2)
     for k in range(Y):
@@ -170,7 +174,9 @@
         return pl.ds(pl.multiple_of(j * HR, HR), HR)
 
     def y1_half(k, j):
-        y1[:, k, :, columns(j)] = dot(xp[k].reshape(NQ * S, LANES), w1[:, columns(j)]).astype(BF).reshape(NQ, S, HR)
+        rows = xp[k].reshape(NQ * S // 2, LANES)
+        for m in range(2):
+            y1[:, k, m * (S // 2):(m + 1) * (S // 2), columns(j)] = dot(rows, w1[m, :, columns(j)]).astype(BF).reshape(NQ, S // 2, HR)
 
     def y1_own(j, u):
         y1_half(c, j)
@@ -239,8 +245,8 @@
     lax.fori_loop(1, NQ, send_y2, 0)
     yp[c, chip] = y2[...]
     lane = lax.broadcasted_iota(jnp.int32, (S, LANES), 1)
-    counted = jnp.sum(xp[...].astype(F32).reshape(Y * CB, LANES), axis=0, keepdims=True)
-    counted = jnp.sum(jnp.where(lane[0:1] == F, counted, 0.0), axis=1, keepdims=True)
+    counted = jnp.sum(xp[...].astype(F32).reshape(Y * CB // 2, LANES), axis=0, keepdims=True)
+    counted = jnp.sum(jnp.where(lane[0:1] % (LANES // 2) == F, counted, 0.0), axis=1, keepdims=True)
     cs[...] = jnp.broadcast_to(counted, (8, LANES))
     cr[z] = cs[...]
     for d in far:
@@ -398,15 +404,19 @@
         send(rcy.at[p, prv, piece(v)], rx2.at[v, 1], ssem.at[E_RX2], rsem_x.at[v, 3], at_x(prv))
 
     def own_x():
-        return jnp.concatenate([xp[m % C, nid * (Y // C) + m // C] for m in range(Y)], axis=0)
+        low_half = lax.broadcasted_iota(jnp.int32, (S // 2, LANES), 1) < LANES // 2
+        for m in range(Y):
+            rows = xp[m % C, nid * (Y // C) + m // C].astype(F32)
+            xn[m * S:m * S + S // 2] = jnp.where(low_half, rows, 0.0).astype(BF)
+            xn[m * S + S // 2:(m + 1) * S] = jnp.where(low_half, turned(rows), 0.0).astype(BF)
 
     def grad_one(v):
         arrived(rx2.at[v, 0], rsem_x.at[v, 2])
         arrived(rx2.at[v, 1], rsem_x.at[v, 3])
         acc = (rcy[v // 2, x, piece(v)] + rx2[v, 0] + rx2[v, 1]).astype(BF)
-        part = dot(acc, own_x())
+        part = dot(acc, xn[...])
         if v >= NV // 2:
-            part = jnp.concatenate([part[:, LANES // 2:], part[:, 0:LANES // 2]], axis=1)
+            part = turned(part)
         per = HU // (Z * 8)
         rows = part.reshape(per, Z, 8, LANES)
         for m in range(per):
@@ -477,7 +487,7 @@
     arrived(mk.at[pl.ds(0, Y - 1)], rsem.at[E_M])
     arrived(dg.at[pl.ds(0, Y - 1)], rsem.at[E_DG])
     steps = [
-        (g_one, 0), (gather_step, 0, 1), (g_one, 1), (gather_step, 1, 1), (g_one, 2), (g_one, 3), (w_begin,),
+        (g_one, 0), (gather_step, 0, 1), (g_one, 1), (gather_step, 1, 1), (g_one, 2), (g_one, 3), (w_begin,), (own_x,),
         (gather_step, 0, 2), (gather_step, 1, 2), (w_core,)]
     for t in range(3, half + 1):
         steps += [(gather_step, 0, t), (gather_step, 1, t)]
@@ -486,8 +496,8 @@
     for t in range(3, half + 1):
         steps += [(gather_step, 2, t), (gather_step, 3, t)]
         if t == 3:
-            steps += [(chunks, 0, 6, 8), (w_x,)]
-    steps += [(reduce_core, 0), (reduce_core, 1), (reduce_x, 0), (reduce_x, 1), (w_y,), (prepare, 1), (chunks, 1, 0, 4), (send_core, 1), (chunks, 1, 4, 8), (reduce_core, 2),
+            steps += [(chunks, 0, 6, 8), (reduce_core, 0), (reduce_core, 1), (w_x,)]
+    steps += [(reduce_x, 0), (reduce_x, 1), (w_y,), (prepare, 1), (chunks, 1, 0, 4), (send_core, 1), (chunks, 1, 4, 8), (reduce_core, 2),
               (reduce_core, 3), (grad_one, 0), (grad_one, 1), (w_z,), (reduce_x, 2), (reduce_x, 3), (o_z,), (grad_one, 2), (grad_one, 3)]
     for step in steps:
         step[0](*step[1:])
@@ -606,11 +616,12 @@
             vm((S, LANES), F32),
             vm((F, H), F32),
             vm((H, NC), F32),
-            vm((LANES, H), BF),
+            vm((2, LANES, H), BF),
             vm((H, LANES), BF),
             vm((LANES, H), BF),
-            vm((S, LANES), BF),
-            vm((C, NQ, S, LANES), BF),
+            vm((S // 2, LANES), BF),
+            vm((C, NQ, S // 2, LANES), BF),
+            vm((NCH, LANES), BF),
             vm((NQ, C, S, H), BF),
             vm((8, LANES), F32),
             vm((Z, 8, LANES), F32),

time: 173 us -> 169 us (0.977)
  Pallas kernels: 169 us -> 166 us
    pallas_call x1, Pallas kernels: 169 us -> 166 us  [device_step(): pl.pallas_call(functools.partial(_step, (Z, Y, X, C, S, CB, H, F, NC)), o...]
where the time goes in v7:
time: 169 us
  Pallas kernels  166 us (98%)
  local copies, waits for them, and re-layouts  2.25 us (1%)
    pallas_call x1, Pallas kernels, device_step(): pl.pallas_call(functools.partial(_step, (Z, Y, X, C, S, CB, H, F, NC)), o...  166 us

profile of v7, /device:TPU:2, one launch (start us, length us, event | category | flops | bytes accessed | tf_op | source)
XLA Modules:
  0.0 169.3 jit_solution(5841649112095020749)
XLA Ops:
  0.6 166.4 %gcn_step.1 = (f32[50,2048]{1,0:T(8,128)S(1)}, f32[2048,121]{1,0:T(8,128)S(1)}, f32[8,128]{1,0:T(8,128)S(1)}) custom-call(bf16[8,4,64,512]{3,2,1,0:T(8,128)(2,1)} %bitcast.5, bf16[50,64]{1,0:T(8,128)(2,1)} %bitcast.6, s32[1,64]{1,0:T(1,128)} %bitcast.7, s32[1,64]{1,0:T(1,128)} %bitcast.8, f32[50,2048]{1,0:T(8,128)} %w_one.1, f32[2048,121]{1,0:T(8,128)} %w_two.1), custom_call_target="tpu_custom_call" | custom-call | tf_op jit(solution)/shard_map/gcn_step/pallas_call | solution.py:686
  167.0 0.5 slice.3
  167.5 0.8 copy.11
  168.3 1.0 copy.12

commit v8 on v7

--- a/solution.py
+++ b/solution.py
@@ -356,43 +356,56 @@
             for k in range(Z):
                 gt[p, piece(v), k * Y * S:(k + 1) * Y * S] = gz[v, k].reshape(Y * S, HU).T
 
-    def chunks(p, lo, hi):
-        def chunk(n, u):
-            k = n % Y
-            core = jnp.where(n < Y, 1 - c, c)
-            yb = lax.rem(y + k + jnp.where(k == 2, 1, 0) - jnp.where(k == 3, 1, 0), Y)
-            off = pl.multiple_of(core * NCH, NCH)
-            dy[p, yb, core] = dot(gt[p], af[yb, :, :, :, pl.ds(off, NCH)].reshape(Z * Y * S, NCH))
-            return u
-
-        if p == 0 and lo < Y <= hi:
-            lax.fori_loop(lo, Y - 1, chunk, 0)
+    nxt, prv, opp = (x + 1) % X, (x + X - 1) % X, (x + 2) % X
+    hh = HU // 2
+
+    def low(v):
+        return pl.ds(v % 2 * HU, hh)
+
+    def high(v):
+        return pl.ds(v % 2 * HU + hh, hh)
+
+    def chunk(p, xb, core):
+        off = pl.multiple_of(core * NCH, NCH)
+        dy[p, xb, core] = dot(gt[p], af[xb, :, :, :, pl.ds(off, NCH)].reshape(Z * Y * S, NCH))
+
+    def send_core(p, k):
+        xb = (x + 2 + k) % X
+        send(dy.at[p, xb, 1 - c], rcy.at[p, xb], ssem.at[E_RC], rsem_c.at[p, k], partner)
+
+    def chunks_far(p):
+        if p == 0:
             for d in (1, 3):
                 for k in range(1, Y):
                     arrived(af.at[0, pl.ds(0, half), 0], rsem_f.at[d // 2, k - 1])
-            lo = Y - 1
-        lax.fori_loop(lo, hi, chunk, 0)
-
-    def send_core(p):
+        chunk(p, opp, 1 - c)
+        send_core(p, 0)
+        chunk(p, opp, c)
+
+    def chunks_rest(p, own):
+        def body(k, u):
+            chunk(p, lax.rem(x + 2 + k, X), c if own else 1 - c)
+            return u
+
+        lax.fori_loop(1, X, body, 0)
+        if not own:
+            for k in range(1, X):
+                send_core(p, k)
+
+    def sum_core(p, k):
+        xb = (x + 2 + k) % X
+        arrived(rcy.at[p, xb], rsem_c.at[p, k])
+        rcy[p, xb] = rcy[p, xb] + dy[p, xb, c]
+
+    def reduce_far(p):
+        sum_core(p, 0)
         for v in (2 * p, 2 * p + 1):
-            send(dy.at[p, :, 1 - c, piece(v)], rcy.at[p, :, piece(v)], ssem.at[E_RC], rsem_c.at[v], partner)
-
-    nxt, prv, opp = (x + 1) % X, (x + X - 1) % X, (x + 2) % X
-    hh = HU // 2
-
-    def low(v):
-        return pl.ds(v % 2 * HU, hh)
-
-    def high(v):
-        return pl.ds(v % 2 * HU + hh, hh)
-
-    def reduce_core(v):
-        p = v // 2
-        arrived(rcy.at[p, :, piece(v)], rsem_c.at[v])
-        for k in range(X):
-            rcy[p, k, piece(v)] = rcy[p, k, piece(v)] + dy[p, k, c, piece(v)]
-        send(rcy.at[p, opp, low(v)], rx1.at[v, 0], ssem.at[E_RX], rsem_x.at[v, 0], at_x(nxt))
-        send(rcy.at[p, opp, high(v)], rx1.at[v, 1], ssem.at[E_RX], rsem_x.at[v, 1], at_x(prv))
+            send(rcy.at[p, opp, low(v)], rx1.at[v, 0], ssem.at[E_RX], rsem_x.at[v, 0], at_x(nxt))
+            send(rcy.at[p, opp, high(v)], rx1.at[v, 1], ssem.at[E_RX], rsem_x.at[v, 1], at_x(prv))
+
+    def reduce_rest(p):
+        for k in range(1, X):
+            sum_core(p, k)
 
     def reduce_x(v):
         p = v // 2
@@ -491,14 +504,15 @@
         (gather_step, 0, 2), (gather_step, 1, 2), (w_core,)]
     for t in range(3, half + 1):
         steps += [(gather_step, 0, t), (gather_step, 1, t)]
-    steps += [(gather_step, 2, 1), (gather_step, 3, 1), (prepare, 0), (chunks, 0, 0, 2), (gather_step, 2, 2), (gather_step, 3, 2),
-              (chunks, 0, 2, 4), (send_core, 0), (chunks, 0, 4, 6)]
+    steps += [(gather_step, 2, 1), (gather_step, 3, 1), (prepare, 0), (chunks_far, 0), (gather_step, 2, 2), (gather_step, 3, 2),
+              (reduce_far, 0), (chunks_rest, 0, False)]
     for t in range(3, half + 1):
         steps += [(gather_step, 2, t), (gather_step, 3, t)]
         if t == 3:
-            steps += [(chunks, 0, 6, 8), (reduce_core, 0), (reduce_core, 1), (w_x,)]
-    steps += [(reduce_x, 0), (reduce_x, 1), (w_y,), (prepare, 1), (chunks, 1, 0, 4), (send_core, 1), (chunks, 1, 4, 8), (reduce_core, 2),
-              (reduce_core, 3), (grad_one, 0), (grad_one, 1), (w_z,), (reduce_x, 2), (reduce_x, 3), (o_z,), (grad_one, 2), (grad_one, 3)]
+            steps += [(chunks_rest, 0, True), (reduce_rest, 0), (w_x,)]
+    steps += [(reduce_x, 0), (reduce_x, 1), (w_y,), (prepare, 1), (chunks_far, 1), (reduce_far, 1), (chunks_rest, 1, False),
+              (chunks_rest, 1, True), (reduce_rest, 1), (grad_one, 0), (grad_one, 1), (w_z,), (reduce_x, 2), (reduce_x, 3), (o_z,),
+              (grad_one, 2), (grad_one, 3)]
     for step in steps:
         step[0](*step[1:])
 
@@ -506,7 +520,6 @@
         xq = (x + d) % X
         send(pb.at[xq], px.at[x], ssem.at[E_PX], rsem.at[E_PX], at_x(xq))
     px[x] = pb[x]
-    o_y()
     arrived(px.at[pl.ds(0, X - 1)], rsem.at[E_PX])
     px[x] = added(px, X)
     for d in far:
@@ -515,12 +528,12 @@
             send(px.at[x, zq], pz.at[c * Z + z], ssem.at[E_PZ], rsem.at[E_PZ], (zq * Y + y, x * C + k))
     send(px.at[x, z], pz.at[c * Z + z], ssem.at[E_PZ], rsem.at[E_PZ], partner)
     pz[c * Z + z] = px[x, z]
+    o_y()
     arrived(pz.at[pl.ds(0, C * Z - 1)], rsem.at[E_PZ])
     pf[...] = added(pz, C * Z)
     for d in far:
         send(pf, qz.at[z], ssem.at[E_QZ], rsem.at[E_QZ], at_z((z + d) % Z))
     qz[z] = pf[...]
-    o_x()
     arrived(qz.at[pl.ds(0, Z - 1)], rsem.at[E_QZ])
     zl, zh = pl.ds(0, half), pl.ds(half, half)
     for d in (2, 1, 3):
@@ -528,20 +541,21 @@
         send(qz.at[zh], qx.at[x], ssem.at[E_QX], rsem.at[E_QX], at_x((x + d) % X))
     qy[y] = qz[zl]
     qx[x] = qz[zh]
+    o_x()
+    arrived(qy.at[pl.ds(0, Y - 1)], rsem.at[E_QY])
+    for d in (2, 1, 3):
+        send(qy, qxy.at[x], ssem.at[E_QXY], rsem.at[E_QXY], at_x((x + d) % X))
+    qxy[x] = qy[...]
+    arrived(qx.at[pl.ds(0, X - 1)], rsem.at[E_QX])
+    for d in (2, 1, 3):
+        send(qx, qyx.at[y], ssem.at[E_QYX], rsem.at[E_QYX], at_y((y + d) % Y))
+    qyx[y] = qx[...]
     arrived(oc.at[0], rsem.at[E_OC])
     for k in range(C):
         full = oc[k].reshape(H // C, LANES)
         dw2_out[k * (H // C):(k + 1) * (H // C), :] = full[:, 0:NC]
         if k == 0:
             loss_out[...] = jnp.broadcast_to(full[0:1, NC:NC + 1] / count, (8, LANES))
-    arrived(qy.at[pl.ds(0, Y - 1)], rsem.at[E_QY])
-    for d in (2, 1, 3):
-        send(qy, qxy.at[x], ssem.at[E_QXY], rsem.at[E_QXY], at_x((x + d) % X))
-    qxy[x] = qy[...]
-    arrived(qx.at[pl.ds(0, X - 1)], rsem.at[E_QX])
-    for d in (2, 1, 3):
-        send(qx, qyx.at[y], ssem.at[E_QYX], rsem.at[E_QYX], at_y((y + d) % Y))
-    qyx[y] = qx[...]
     arrived(qxy.at[pl.ds(0, X - 1)], rsem.at[E_QXY])
     arrived(qyx.at[pl.ds(0, Y - 1)], rsem.at[E_QYX])
     for yb in range(Y):
@@ -677,7 +691,7 @@
             dma((2, Y - 1)),
             dma((2 * NSUB, Z - 1)),
             dma((NV, 2, Z // 2 + 1)),
-            dma((NV,)),
+            dma((NV // 2, X)),
             dma((NV, 4)),
         ]
         vspec = pl.BlockSpec(memory_space=pltpu.VMEM)

time: 169 us -> 167 us (0.988)
  Pallas kernels: 166 us -> 164 us
    pallas_call x1, Pallas kernels: 166 us -> 164 us  [device_step(): pl.pallas_call(functools.partial(_step, (Z, Y, X, C, S, CB, H, F, NC)), o...]
where the time goes in v8:
time: 167 us
  Pallas kernels  164 us (98%)
  local copies, waits for them, and re-layouts  2.25 us (1%)
    pallas_call x1, Pallas kernels, device_step(): pl.pallas_call(functools.partial(_step, (Z, Y, X, C, S, CB, H, F, NC)), o...  164 us

profile of v8, /device:TPU:2, one launch (start us, length us, event | category | flops | bytes accessed | tf_op | source)
XLA Modules:
  0.0 167.1 jit_solution(4302054480150404640)
XLA Ops:
  0.6 164.2 %gcn_step.1 = (f32[50,2048]{1,0:T(8,128)S(1)}, f32[2048,121]{1,0:T(8,128)S(1)}, f32[8,128]{1,0:T(8,128)S(1)}) custom-call(bf16[8,4,64,512]{3,2,1,0:T(8,128)(2,1)} %bitcast.5, bf16[50,64]{1,0:T(8,128)(2,1)} %bitcast.6, s32[1,64]{1,0:T(1,128)} %bitcast.7, s32[1,64]{1,0:T(1,128)} %bitcast.8, f32[50,2048]{1,0:T(8,128)} %w_one.1, f32[2048,121]{1,0:T(8,128)} %w_two.1), custom_call_target="tpu_custom_call" | custom-call | tf_op jit(solution)/shard_map/gcn_step/pallas_call | solution.py:700
  164.8 0.5 slice.3
  165.3 0.8 copy.11
  166.1 1.0 copy.12

commit v9 on v8

--- a/solution.py
+++ b/solution.py
@@ -403,6 +403,17 @@
             send(rcy.at[p, opp, low(v)], rx1.at[v, 0], ssem.at[E_RX], rsem_x.at[v, 0], at_x(nxt))
             send(rcy.at[p, opp, high(v)], rx1.at[v, 1], ssem.at[E_RX], rsem_x.at[v, 1], at_x(prv))
 
+    def far_and_rest(p):
+        @pl.when(c == 0)
+        def _():
+            reduce_far(p)
+            chunks_rest(p, False)
+
+        @pl.when(c == 1)
+        def _():
+            chunks_rest(p, False)
+            reduce_far(p)
+
     def reduce_rest(p):
         for k in range(1, X):
             sum_core(p, k)
@@ -501,18 +512,13 @@
     arrived(dg.at[pl.ds(0, Y - 1)], rsem.at[E_DG])
     steps = [
         (g_one, 0), (gather_step, 0, 1), (g_one, 1), (gather_step, 1, 1), (g_one, 2), (g_one, 3), (w_begin,), (own_x,),
-        (gather_step, 0, 2), (gather_step, 1, 2), (w_core,)]
-    for t in range(3, half + 1):
-        steps += [(gather_step, 0, t), (gather_step, 1, t)]
-    steps += [(gather_step, 2, 1), (gather_step, 3, 1), (prepare, 0), (chunks_far, 0), (gather_step, 2, 2), (gather_step, 3, 2),
-              (reduce_far, 0), (chunks_rest, 0, False)]
-    for t in range(3, half + 1):
-        steps += [(gather_step, 2, t), (gather_step, 3, t)]
-        if t == 3:
-            steps += [(chunks_rest, 0, True), (reduce_rest, 0), (w_x,)]
-    steps += [(reduce_x, 0), (reduce_x, 1), (w_y,), (prepare, 1), (chunks_far, 1), (reduce_far, 1), (chunks_rest, 1, False),
-              (chunks_rest, 1, True), (reduce_rest, 1), (grad_one, 0), (grad_one, 1), (w_z,), (reduce_x, 2), (reduce_x, 3), (o_z,),
-              (grad_one, 2), (grad_one, 3)]
+        (gather_step, 0, 2), (gather_step, 1, 2), (w_core,), (gather_step, 2, 1),
+        (gather_step, 0, 3), (gather_step, 1, 3), (gather_step, 3, 1),
+        (gather_step, 0, 4), (gather_step, 1, 4), (gather_step, 2, 2), (gather_step, 3, 2),
+        (prepare, 0), (chunks_far, 0), (far_and_rest, 0), (gather_step, 2, 3), (gather_step, 3, 3),
+        (chunks_rest, 0, True), (reduce_rest, 0), (reduce_x, 0), (reduce_x, 1), (gather_step, 2, 4), (gather_step, 3, 4), (w_x,),
+        (prepare, 1), (chunks_far, 1), (far_and_rest, 1), (w_y,), (chunks_rest, 1, True), (reduce_rest, 1), (grad_one, 0), (grad_one, 1),
+        (reduce_x, 2), (reduce_x, 3), (w_z,), (grad_one, 2), (o_z,), (grad_one, 3)]
     for step in steps:
         step[0](*step[1:])
 
@@ -618,7 +624,7 @@
         HB = H // Y
         HU = HB // NV
         NCH = Y * S
-        assert R == Z * Y and CB == S * I and X == Y and F + 2 <= LANES // 2 and NC < LANES
+        assert R == Z * Y and CB == S * I and X == Y and Z == 8 and F + 2 <= LANES // 2 and NC < LANES
         vm = pltpu.VMEM
         dma = pltpu.SemaphoreType.DMA
         scratch = [

time: 167 us -> 166 us (level)
  no operation moved by 1% of the time
where the time goes in v9:
time: 166 us
  Pallas kernels  163 us (98%)
  local copies, waits for them, and re-layouts  2.25 us (1%)
    pallas_call x1, Pallas kernels, device_step(): pl.pallas_call(functools.partial(_step, (Z, Y, X, C, S, CB, H, F, NC)), o...  163 us

profile of v9, /device:TPU:2, one launch (start us, length us, event | category | flops | bytes accessed | tf_op | source)
XLA Modules:
  0.0 166.2 jit_solution(16729326068936398048)
XLA Ops:
  0.6 163.3 %gcn_step.1 = (f32[50,2048]{1,0:T(8,128)S(1)}, f32[2048,121]{1,0:T(8,128)S(1)}, f32[8,128]{1,0:T(8,128)S(1)}) custom-call(bf16[8,4,64,512]{3,2,1,0:T(8,128)(2,1)} %bitcast.5, bf16[50,64]{1,0:T(8,128)(2,1)} %bitcast.6, s32[1,64]{1,0:T(1,128)} %bitcast.7, s32[1,64]{1,0:T(1,128)} %bitcast.8, f32[50,2048]{1,0:T(8,128)} %w_one.1, f32[2048,121]{1,0:T(8,128)} %w_two.1), custom_call_target="tpu_custom_call" | custom-call | tf_op jit(solution)/shard_map/gcn_step/pallas_call | solution.py:706
  163.9 0.5 slice.3
  164.5 0.8 copy.11
  165.2 1.0 copy.12

commit v10 on v9

--- a/solution.py
+++ b/solution.py
@@ -407,10 +407,16 @@
         @pl.when(c == 0)
         def _():
             reduce_far(p)
+            if p == 0:
+                gather_step(2, 3)
+                gather_step(3, 3)
             chunks_rest(p, False)
 
         @pl.when(c == 1)
         def _():
+            if p == 0:
+                gather_step(2, 3)
+                gather_step(3, 3)
             chunks_rest(p, False)
             reduce_far(p)
 
@@ -515,8 +521,8 @@
         (gather_step, 0, 2), (gather_step, 1, 2), (w_core,), (gather_step, 2, 1),
         (gather_step, 0, 3), (gather_step, 1, 3), (gather_step, 3, 1),
         (gather_step, 0, 4), (gather_step, 1, 4), (gather_step, 2, 2), (gather_step, 3, 2),
-        (prepare, 0), (chunks_far, 0), (far_and_rest, 0), (gather_step, 2, 3), (gather_step, 3, 3),
-        (chunks_rest, 0, True), (reduce_rest, 0), (reduce_x, 0), (reduce_x, 1), (gather_step, 2, 4), (gather_step, 3, 4), (w_x,),
+        (prepare, 0), (chunks_far, 0), (far_and_rest, 0),
+        (chunks_rest, 0, True), (gather_step, 2, 4), (reduce_rest, 0), (reduce_x, 0), (gather_step, 3, 4), (reduce_x, 1), (w_x,),
         (prepare, 1), (chunks_far, 1), (far_and_rest, 1), (w_y,), (chunks_rest, 1, True), (reduce_rest, 1), (grad_one, 0), (grad_one, 1),
         (reduce_x, 2), (reduce_x, 3), (w_z,), (grad_one, 2), (o_z,), (grad_one, 3)]
     for step in steps:

time: 166 us -> 165 us (level)
  no operation moved by 1% of the time
where the time goes in v10:
time: 165 us
  Pallas kernels  162 us (98%)
  local copies, waits for them, and re-layouts  2.25 us (1%)
    pallas_call x1, Pallas kernels, device_step(): pl.pallas_call(functools.partial(_step, (Z, Y, X, C, S, CB, H, F, NC)), o...  162 us

profile of v10, /device:TPU:2, one launch (start us, length us, event | category | flops | bytes accessed | tf_op | source)
XLA Modules:
  0.0 164.7 jit_solution(629326209969908675)
XLA Ops:
  0.6 161.8 %gcn_step.1 = (f32[50,2048]{1,0:T(8,128)S(1)}, f32[2048,121]{1,0:T(8,128)S(1)}, f32[8,128]{1,0:T(8,128)S(1)}) custom-call(bf16[8,4,64,512]{3,2,1,0:T(8,128)(2,1)} %bitcast.5, bf16[50,64]{1,0:T(8,128)(2,1)} %bitcast.6, s32[1,64]{1,0:T(1,128)} %bitcast.7, s32[1,64]{1,0:T(1,128)} %bitcast.8, f32[50,2048]{1,0:T(8,128)} %w_one.1, f32[2048,121]{1,0:T(8,128)} %w_two.1), custom_call_target="tpu_custom_call" | custom-call | tf_op jit(solution)/shard_map/gcn_step/pallas_call | solution.py:712
  162.5 0.5 slice.3
  163.0 0.8 copy.11
  163.7 1.0 copy.12

commit v11 on v10

--- a/solution.py
+++ b/solution.py
@@ -136,16 +136,16 @@
         for d in (2, 1, 3):
             yq = (y + d) % Y
             send(af.at[y, zc, yq], af.at[y, zc, yq], ssem.at[E_A], rsem_a.at[d - 1, zc], at_y(yq))
-    def spread_a(k):
+    def spread_a(k, lo, n, slot):
         for d in (1, 3):
             yq = (y + d) % Y
-            ya = (yq + k) % Y
-            send(af.at[y, :, ya], af.at[y, :, ya], ssem.at[E_B], rsem_b.at[d // 2, k - 1], at_y(yq))
+            ref = af.at[y, pl.ds(lo, n), (yq + k) % Y]
+            send(ref, ref, ssem.at[E_B], rsem_b.at[d // 2, slot], at_y(yq))
 
     def forward_a():
-        for k in range(1, Y):
-            for d in (1, 3):
-                arrived(af.at[0, :, 0], rsem_b.at[d // 2, k - 1])
+        for d in (1, 3):
+            for slot, n in enumerate((Z, Z, half, half)):
+                arrived(af.at[0, pl.ds(0, n), 0], rsem_b.at[d // 2, slot])
         for k in range(1, Y):
             for d in (1, 3):
                 ys, yq = (y - d + Y) % Y, (y + d) % Y
@@ -153,8 +153,9 @@
                 ya = (yq + k) % Y
                 send(af.at[ys, pl.ds(lo, half), ya], af.at[ys, pl.ds(lo, half), ya], ssem.at[E_F], rsem_f.at[d // 2, k - 1], at_y(yq))
 
-    spread_a(1)
-    spread_a(2)
+    spread_a(1, 0, Z, 0)
+    spread_a(2, 0, Z, 1)
+    spread_a(3, 0, half, 2)
 
     load_1.wait()
     w1[...] = jnp.zeros_like(w1)
@@ -271,7 +272,7 @@
         yq = (y + d) % Y
         send(ms.at[yq], mk.at[y], ssem.at[E_M], rsem.at[E_M], at_y(yq))
     mk[y] = ms[y]
-    spread_a(3)
+    spread_a(3, half, half, 3)
     arrived(zr.at[pl.ds(0, Z - 1)], rsem.at[E_Z2])
     z2 = added(zr, Z)
 
@@ -699,7 +700,7 @@
             dma((NSEM,)),
             dma((NSEM,)),
             dma((Y - 1, Z)),
-            dma((2, Y - 1)),
+            dma((2, 4)),
             dma((2, Y - 1)),
             dma((2 * NSUB, Z - 1)),
             dma((NV, 2, Z // 2 + 1)),

time: 165 us -> 165 us (level)
  no operation moved by 1% of the time
where the time goes in v11:
time: 165 us
  Pallas kernels  162 us (98%)
  local copies, waits for them, and re-layouts  2.25 us (1%)
    pallas_call x1, Pallas kernels, device_step(): pl.pallas_call(functools.partial(_step, (Z, Y, X, C, S, CB, H, F, NC)), o...  162 us

profile of v11, /device:TPU:2, one launch (start us, length us, event | category | flops | bytes accessed | tf_op | source)
XLA Modules:
  0.0 164.7 jit_solution(9996768243974539341)
XLA Ops:
  0.6 161.8 %gcn_step.1 = (f32[50,2048]{1,0:T(8,128)S(1)}, f32[2048,121]{1,0:T(8,128)S(1)}, f32[8,128]{1,0:T(8,128)S(1)}) custom-call(bf16[8,4,64,512]{3,2,1,0:T(8,128)(2,1)} %bitcast.5, bf16[50,64]{1,0:T(8,128)(2,1)} %bitcast.6, s32[1,64]{1,0:T(1,128)} %bitcast.7, s32[1,64]{1,0:T(1,128)} %bitcast.8, f32[50,2048]{1,0:T(8,128)} %w_one.1, f32[2048,121]{1,0:T(8,128)} %w_two.1), custom_call_target="tpu_custom_call" | custom-call | tf_op jit(solution)/shard_map/gcn_step/pallas_call | solution.py:713
  162.5 0.5 slice.3
  163.0 0.8 copy.11
  163.8 1.0 copy.12
